TPU v7x, 256 devices: a whole 4x4x8 slice. The times are simulated.
256 devices in a mesh: gx: 32 (over z, y), gy: 8 (over x, core).
Axes of the slice: x: 4, y: 4, z: 8, core: 2. Of those that a mesh axis runs over, the one named last changes fastest.
Arguments:
- right_side: float32 [256, 512, 128], P('gy', 'gx'), may hold values from -6 to 9
- diagonal: float32 [256, 512, 128], P('gy', 'gx'), may hold values from 0.02 to 0.5
- horizontal: float32 [256, 512, 128], P('gy', 'gx'), may hold values from 0.1 to 1
- vertical: float32 [128], replicated, may hold values from 0.2 to 2
- precond: float32 [2, 128, 128], replicated, may hold values from -4 to 4
- edge_rows: int32 [2, 256], replicated, may hold values from 0 to 255, as said below
Outputs:
- solution_field: float32 [256, 512, 128], P('gy', 'gx')
- residual: float32 [256, 512, 128], P('gy', 'gx')
- residual_sq: float32 [3], replicated
Inputs may be any that keep to these rules, and one draw needn't show every extreme that they name: Each row of edge_rows lists every number 0 to 255 exactly once.
All inputs are finite; a program needn't handle non-finite values.
Results may differ from a plain program's by a relative error of at most 0.00014.
Values sent between devices are 32-bit elements; how exact they have to be, the bound alone decides.
A program may use at most 64 MiB of HBM per device.

v0:
```python
import jax
import jax.numpy as jnp
from jax import lax
from jax.sharding import Mesh
from jax.sharding import PartitionSpec as P

ITERS = 3
GX = ("gx_0", "gx_1")
GY = ("gy_0", "gy_1")


def padded(x, sides, width, wrap):
    for axis, dim in sides:
        devices, length = (lax.axis_size(axis), x.shape[dim])
        up = [(i, (i + 1) % devices) for i in range(devices if wrap else devices - 1)]
        down = [(j, i) for i, j in up]
        last = lax.slice_in_dim(x, length - width, length, axis=dim)
        initial = lax.slice_in_dim(x, 0, width, axis=dim)
        before = lax.ppermute(last, axis, up)
        after = lax.ppermute(initial, axis, down)
        x = jnp.concatenate([before, x, after], axis=dim)
    return x


def in_order(blocks, dim):
    blocks = jnp.moveaxis(blocks, 0, dim)
    dims = blocks.shape
    return blocks.reshape(*dims[:dim], dims[dim] * dims[dim + 1], *dims[dim + 2 :])


def from_everyone(x, axis):
    copies = jnp.broadcast_to(x, (lax.axis_size(axis), *x.shape))
    return lax.all_to_all(copies, axis, split_axis=0, concat_axis=0, tiled=True)


def gathered_copies(x, axis, dim):
    return in_order(from_everyone(x, axis), dim)


def over_copies(x, axis):
    everything = from_everyone(x, axis)
    return jnp.sum(everything, axis=0)


def over_axes(x, axes):
    far, near = axes
    return over_copies(over_copies(x, near), far)


def local_product(left, right):
    return jnp.sum(left * right)


def on_device(right_side, diagonal, horizontal, vertical, precond, edge_rows):
    rows, cols, levels = right_side.shape
    n_gx = lax.axis_size(GX)
    n_gy = lax.axis_size(GY)
    col_index = lax.axis_index(GX)
    row_index = lax.axis_index(GY)
    total_cells = float(rows * cols * levels * n_gx * n_gy)
    half = n_gx // 2
    panel = (col_index >= half).astype(jnp.int32)
    matrix = lax.dynamic_index_in_dim(precond, panel, 0, keepdims=False)
    east_table = jnp.where(col_index == half - 1, edge_rows[0], edge_rows[1])
    west_table = jnp.where(col_index == half, edge_rows[0], edge_rows[1])
    first_row = row_index * rows
    east_local = lax.dynamic_slice_in_dim(east_table, first_row, rows)
    west_local = lax.dynamic_slice_in_dim(west_table, first_row, rows)
    east_border = (col_index == half - 1) | (col_index == n_gx - 1)
    west_border = (col_index == half) | (col_index == 0)
    solution_field = jnp.zeros_like(right_side)
    residual = right_side
    directions = []
    images = []
    norms = []
    for step in range(ITERS):
        pre = jnp.einsum("yxl,kl->yxk", residual, matrix, precision=lax.Precision.HIGHEST)
        wide = padded(pre, ((GX, 1),), 1, True)
        edges = jnp.stack([wide[:, 0], wide[:, -1]], 0)
        whole = gathered_copies(edges, GY, 1)
        west_fix = jnp.take(whole[0], west_local, axis=0)
        east_fix = jnp.take(whole[1], east_local, axis=0)
        west = jnp.where(west_border, west_fix, edges[0])
        east = jnp.where(east_border, east_fix, edges[1])
        tall = padded(pre, ((GY, 0),), 1, False)
        flat = jnp.pad(pre, ((0, 0), (0, 0), (1, 1)))
        east_side = jnp.concatenate([pre[:, 1:], east[:, None]], 1)
        west_side = jnp.concatenate([west[:, None], pre[:, :-1]], 1)
        beside = east_side + west_side + tall[2:] + tall[:-2]
        column = flat[:, :, 2:] + flat[:, :, :-2]
        image = diagonal * pre + horizontal * (4.0 * pre - beside) + vertical * (2.0 * pre - column)
        count = len(images)
        terms = [local_product(image, older) for older in images]
        terms = terms + [local_product(residual, older) for older in images]
        terms = terms + [local_product(image, image), local_product(residual, image)]
        if step > 0:
            terms.append(local_product(residual, residual))
        totals = over_axes(jnp.stack(terms), (("gx_0", "gx_1"), ("gy_0", "gy_1"))) / total_cells
        coeffs = totals[:count]
        against = totals[count : 2 * count]
        square = totals[2 * count] - jnp.sum(coeffs * coeffs)
        along = totals[2 * count + 1] - jnp.sum(coeffs * against)
        if step > 0:
            norms.append(totals[2 * count + 2])
        for number in range(count):
            pre = pre - coeffs[number] * directions[number]
            image = image - coeffs[number] * images[number]
        scale = 1.0 / jnp.sqrt(square)
        alpha = along * scale
        direction = pre * scale
        image = image * scale
        solution_field = solution_field + alpha * direction
        residual = residual - alpha * image
        directions.append(direction)
        images.append(image)
    norms.append(
        over_axes(local_product(residual, residual), (("gx_0", "gx_1"), ("gy_0", "gy_1")))
        / total_cells
    )
    return (solution_field, residual, jnp.stack(norms))


def solution(mesh):
    split = Mesh(mesh.devices.reshape(8, 4, 4, 2), ("gx_0", "gx_1", "gy_0", "gy_1"))
    in_specs = (P(GY, GX, None), P(GY, GX, None), P(GY, GX, None), P(), P(), P())
    out_specs = (P(GY, GX, None), P(GY, GX, None), P())
    return jax.shard_map(
        on_device, mesh=split, in_specs=in_specs, out_specs=out_specs, check_vma=False
    )
```

profile of v0, /device:TPU:1, one launch (start us, length us, event | category | flops | bytes accessed | tf_op | source)
XLA Modules:
  0.0 197.2 jit_solution(12692663423088850675)
XLA Ops:
  2.9 5.1 %collective-permute-start.2 = (f32[1,16,128]{2,0,1:T(1,128)S(1)}, f32[1,16,128]{2,0,1:T(1,128)S(1)}, u32[]{:S(2)}, u32[]{:S(2)}) collective-permute-start(f32[1,16,128]{2,0,1:T(1,128)S(1)} %get-tuple-element.68), channel_id=1, source_target_pairs={{1,0},{2,1},{3,2},{4,3},{5,4},{6,5},{7,6},{9,8},{10,9},{11,10},{12... | collective-permute-start | bytes 24584 | tf_op jit(solution)/shard_map/ppermute | solution.py:20
  10.0 7.5 %collective-permute-start.1 = (f32[32,1,128]{2,0,1:T(8,128)S(1)}, f32[32,1,128]{2,0,1:T(8,128)S(1)}, u32[]{:S(2)}, u32[]{:S(2)}) collective-permute-start(f32[32,1,128]{2,0,1:T(8,128)S(1)} %get-tuple-element.66), channel_id=1, source_target_pairs={{8,0},{16,8},{24,16},{32,24},{40,32},{48,40},{56,48},{64,56},{72,6... | collective-permute-start | bytes 49160 | tf_op jit(solution)/shard_map/ppermute | solution.py:20
  18.3 5.4 %collective-permute-done = f32[32,1,128]{2,0,1:T(8,128)S(1)} collective-permute-done((f32[32,1,128]{2,0,1:T(8,128)S(1)}, f32[32,1,128]{2,0,1:T(8,128)S(1)}, u32[]{:S(2)}, u32[]{:S(2)}) %collective-permute-start) | collective-permute-done | bytes 16416 | tf_op jit(solution)/shard_map/ppermute | solution.py:19
  24.4 4.8 %all-to-all-start = ((f32[8,2,32,128]{3,2,1,0:T(8,128)}), f32[8,2,32,128]{3,2,1,0:T(8,128)S(1)}, u32[]{:S(2)}, u32[]{:S(2)}) async-start(f32[8,2,32,128]{3,2,1,0:T(8,128)} %broadcast_in_dim.63), calls=%async_computation | async-start | bytes 524288 | tf_op jit(solution)/shard_map/all_to_all | solution.py:33
  29.3 6.4 %all-to-all-done = f32[8,2,32,128]{3,2,1,0:T(8,128)S(1)} async-done(((f32[8,2,32,128]{3,2,1,0:T(8,128)}), f32[8,2,32,128]{3,2,1,0:T(8,128)S(1)}, u32[]{:S(2)}, u32[]{:S(2)}) %all-to-all-start) | async-done | bytes 262176 | tf_op jit(solution)/shard_map/all_to_all | solution.py:33
  40.3 8.0 %all_to_all.63 = f32[8,1,2]{2,1,0:T(1,128)S(1)} all-to-all(f32[8,1,2]{2,1,0:T(1,128)S(1)} %broadcast_in_dim.66), channel_id=1, replica_groups=mesh['gx_0'=8,'gx_1'=4,'gy_0'=4,'gy_1'=2] {'gy_0','gy_1'}, dimensions={0} | all-to-all | bytes 128 | tf_op jit(solution)/shard_map/all_to_all | solution.py:33
  48.3 11.6 %all_to_all.64 = f32[32,1,2]{2,1,0:T(1,128)S(1)} all-to-all(f32[32,1,2]{2,1,0:T(1,128)S(1)} %broadcast_in_dim.67), channel_id=1, replica_groups=mesh['gx_0'=8,'gx_1'=4,'gy_0'=4,'gy_1'=2] {'gx_0','gx_1'}, dimensions={0} | all-to-all | bytes 512 | tf_op jit(solution)/shard_map/all_to_all | solution.py:33
  63.9 4.3 %collective-permute-start.6 = (f32[1,16,128]{2,0,1:T(1,128)S(1)}, f32[1,16,128]{2,0,1:T(1,128)S(1)}, u32[]{:S(2)}, u32[]{:S(2)}) collective-permute-start(f32[1,16,128]{2,0,1:T(1,128)S(1)} %get-tuple-element.60), channel_id=1, source_target_pairs={{1,0},{2,1},{3,2},{4,3},{5,4},{6,5},{7,6},{9,8},{10,9},{11,10},{12... | collective-permute-start | bytes 24584 | tf_op jit(solution)/shard_map/ppermute | solution.py:20
  68.2 2.1 %collective-permute-start.7 = (f32[1,16,128]{2,0,1:T(1,128)S(1)}, f32[1,16,128]{2,0,1:T(1,128)S(1)}, u32[]{:S(2)}, u32[]{:S(2)}) collective-permute-start(f32[1,16,128]{2,0,1:T(1,128)S(1)} %get-tuple-element.61), channel_id=1, source_target_pairs={{0,1},{1,2},{2,3},{3,4},{4,5},{5,6},{6,7},{8,9},{9,10},{10,11},{11... | collective-permute-start | bytes 24584 | tf_op jit(solution)/shard_map/ppermute | solution.py:19
  71.1 5.5 %all-to-all-start.3 = ((f32[8,2,32,128]{3,2,1,0:T(8,128)}), f32[8,2,32,128]{3,2,1,0:T(8,128)S(1)}, u32[]{:S(2)}, u32[]{:S(2)}) async-start(f32[8,2,32,128]{3,2,1,0:T(8,128)} %broadcast_in_dim.68), calls=%async_computation.3 | async-start | bytes 524288 | tf_op jit(solution)/shard_map/all_to_all | solution.py:33
  76.6 6.4 %all-to-all-done.3 = f32[8,2,32,128]{3,2,1,0:T(8,128)S(1)} async-done(((f32[8,2,32,128]{3,2,1,0:T(8,128)}), f32[8,2,32,128]{3,2,1,0:T(8,128)S(1)}, u32[]{:S(2)}, u32[]{:S(2)}) %all-to-all-start.3) | async-done | bytes 262176 | tf_op jit(solution)/shard_map/all_to_all | solution.py:33
  85.6 3.3 %stack.76 = f32[5]{0:T(128)S(1)} concatenate(f32[1]{0:T(128)} %bitcast.27, f32[1]{0:T(128)} %bitcast.28, f32[1]{0:T(128)} %bitcast.29, f32[1]{0:T(128)} %bitcast.30, f32[1]{0:T(128)} %bitcast.31), dimensions={0} | concatenate | bytes 40 | tf_op jit(solution)/shard_map/stack | solution.py:98
  88.8 8.0 %all_to_all.65 = f32[8,1,5]{2,1,0:T(1,128)S(1)} all-to-all(f32[8,1,5]{2,1,0:T(1,128)S(1)} %broadcast_in_dim.71), channel_id=1, replica_groups=mesh['gx_0'=8,'gx_1'=4,'gy_0'=4,'gy_1'=2] {'gy_0','gy_1'}, dimensions={0} | all-to-all | bytes 320 | tf_op jit(solution)/shard_map/all_to_all | solution.py:33
  96.9 12.6 %all_to_all.66 = f32[32,1,5]{2,1,0:T(1,128)S(1)} all-to-all(f32[32,1,5]{2,1,0:T(1,128)S(1)} %broadcast_in_dim.72), channel_id=1, replica_groups=mesh['gx_0'=8,'gx_1'=4,'gy_0'=4,'gy_1'=2] {'gx_0','gx_1'}, dimensions={0} | all-to-all | bytes 1280 | tf_op jit(solution)/shard_map/all_to_all | solution.py:33
  116.8 4.6 %collective-permute-start.10 = (f32[1,16,128]{2,0,1:T(1,128)S(1)}, f32[1,16,128]{2,0,1:T(1,128)S(1)}, u32[]{:S(2)}, u32[]{:S(2)}) collective-permute-start(f32[1,16,128]{2,0,1:T(1,128)S(1)} %get-tuple-element.52), channel_id=1, source_target_pairs={{1,0},{2,1},{3,2},{4,3},{5,4},{6,5},{7,6},{9,8},{10,9},{11,10},{12... | collective-permute-start | bytes 24584 | tf_op jit(solution)/shard_map/ppermute | solution.py:20
  121.4 2.1 %collective-permute-start.11 = (f32[1,16,128]{2,0,1:T(1,128)S(1)}, f32[1,16,128]{2,0,1:T(1,128)S(1)}, u32[]{:S(2)}, u32[]{:S(2)}) collective-permute-start(f32[1,16,128]{2,0,1:T(1,128)S(1)} %get-tuple-element.53), channel_id=1, source_target_pairs={{0,1},{1,2},{2,3},{3,4},{4,5},{5,6},{6,7},{8,9},{9,10},{10,11},{11... | collective-permute-start | bytes 24584 | tf_op jit(solution)/shard_map/ppermute | solution.py:19
  124.3 5.5 %all-to-all-start.6 = ((f32[8,2,32,128]{3,2,1,0:T(8,128)}), f32[8,2,32,128]{3,2,1,0:T(8,128)S(1)}, u32[]{:S(2)}, u32[]{:S(2)}) async-start(f32[8,2,32,128]{3,2,1,0:T(8,128)} %broadcast_in_dim.73), calls=%async_computation.6 | async-start | bytes 524288 | tf_op jit(solution)/shard_map/all_to_all | solution.py:33
  129.8 6.4 %all-to-all-done.6 = f32[8,2,32,128]{3,2,1,0:T(8,128)S(1)} async-done(((f32[8,2,32,128]{3,2,1,0:T(8,128)}), f32[8,2,32,128]{3,2,1,0:T(8,128)S(1)}, u32[]{:S(2)}, u32[]{:S(2)}) %all-to-all-start.6) | async-done | bytes 262176 | tf_op jit(solution)/shard_map/all_to_all | solution.py:33
  138.7 4.5 %stack.85 = f32[7]{0:T(128)S(1)} concatenate(f32[1]{0:T(128)} %bitcast.44, f32[1]{0:T(128)} %bitcast.45, f32[1]{0:T(128)} %bitcast.46, f32[1]{0:T(128)} %bitcast.47, f32[1]{0:T(128)} %bitcast.48, f32[1]{0:T(128)} %bitcast.49, f32[1]{0:T(128)} %bitcast.50), dimensions={0} | concatenate | bytes 56 | tf_op jit(solution)/shard_map/stack | solution.py:98
  143.3 8.0 %all_to_all.67 = f32[8,1,7]{2,1,0:T(1,128)S(1)} all-to-all(f32[8,1,7]{2,1,0:T(1,128)S(1)} %broadcast_in_dim.76), channel_id=1, replica_groups=mesh['gx_0'=8,'gx_1'=4,'gy_0'=4,'gy_1'=2] {'gy_0','gy_1'}, dimensions={0} | all-to-all | bytes 448 | tf_op jit(solution)/shard_map/all_to_all | solution.py:33
  151.3 12.6 %all_to_all.68 = f32[32,1,7]{2,1,0:T(1,128)S(1)} all-to-all(f32[32,1,7]{2,1,0:T(1,128)S(1)} %broadcast_in_dim.77), channel_id=1, replica_groups=mesh['gx_0'=8,'gx_1'=4,'gy_0'=4,'gy_1'=2] {'gx_0','gx_1'}, dimensions={0} | all-to-all | bytes 1792 | tf_op jit(solution)/shard_map/all_to_all | solution.py:33
  170.7 9.1 %all_to_all.69 = f32[8,1,1]{2,1,0:T(1,128)S(1)} all-to-all(f32[8,1,1]{2,1,0:T(1,128)S(1)} %broadcast_in_dim.78), channel_id=1, replica_groups=mesh['gx_0'=8,'gx_1'=4,'gy_0'=4,'gy_1'=2] {'gy_0','gy_1'}, dimensions={0} | all-to-all | bytes 64 | tf_op jit(solution)/shard_map/all_to_all | solution.py:33
  181.7 3.9 %all-to-all-start.10 = ((f32[32,1,1]{2,1,0:T(1,128)}), f32[32,1,1]{2,1,0:T(1,128)S(1)}, u32[]{:S(2)}, u32[]{:S(2)}) async-start(f32[32,1,1]{2,1,0:T(1,128)} %broadcast_in_dim.79), calls=%async_computation.10 | async-start | bytes 32768 | tf_op jit(solution)/shard_map/all_to_all | solution.py:33
  189.3 4.8 %all-to-all-done.10 = f32[32,1,1]{2,1,0:T(1,128)S(1)} async-done(((f32[32,1,1]{2,1,0:T(1,128)}), f32[32,1,1]{2,1,0:T(1,128)S(1)}, u32[]{:S(2)}, u32[]{:S(2)}) %all-to-all-start.10) | async-done | bytes 160 | tf_op jit(solution)/shard_map/all_to_all | solution.py:33
  (99 shorter events, 35.2 us)
Async XLA Ops:
  0.6 0.9 copy-start
  2.9 34.1 %collective-permute-start.2 = (f32[1,16,128]{2,0,1:T(1,128)S(1)}, f32[1,16,128]{2,0,1:T(1,128)S(1)}, u32[]{:S(2)}, u32[]{:S(2)}) collective-permute-start(f32[1,16,128]{2,0,1:T(1,128)S(1)} %get-tuple-element.68), channel_id=1, source_target_pairs={{1,0},{2,1},{3,2},{4,3},{5,4},{6,5},{7,6},{9,8},{10,9},{11,10},{12... | collective-permute-start | bytes 24584 | tf_op jit(solution)/shard_map/ppermute | solution.py:20
  8.0 29.0 %collective-permute-start.3 = (f32[1,16,128]{2,0,1:T(1,128)S(1)}, f32[1,16,128]{2,0,1:T(1,128)S(1)}, u32[]{:S(2)}, u32[]{:S(2)}) collective-permute-start(f32[1,16,128]{2,0,1:T(1,128)S(1)} %get-tuple-element.69), channel_id=1, source_target_pairs={{0,1},{1,2},{2,3},{3,4},{4,5},{5,6},{6,7},{8,9},{9,10},{10,11},{11... | collective-permute-start | bytes 24584 | tf_op jit(solution)/shard_map/ppermute | solution.py:19
  10.0 8.4 %collective-permute-start.1 = (f32[32,1,128]{2,0,1:T(8,128)S(1)}, f32[32,1,128]{2,0,1:T(8,128)S(1)}, u32[]{:S(2)}, u32[]{:S(2)}) collective-permute-start(f32[32,1,128]{2,0,1:T(8,128)S(1)} %get-tuple-element.66), channel_id=1, source_target_pairs={{8,0},{16,8},{24,16},{32,24},{40,32},{48,40},{56,48},{64,56},{72,6... | collective-permute-start | bytes 49160 | tf_op jit(solution)/shard_map/ppermute | solution.py:20
  17.4 6.2 %collective-permute-start = (f32[32,1,128]{2,0,1:T(8,128)S(1)}, f32[32,1,128]{2,0,1:T(8,128)S(1)}, u32[]{:S(2)}, u32[]{:S(2)}) collective-permute-start(f32[32,1,128]{2,0,1:T(8,128)S(1)} %get-tuple-element.67), channel_id=1, source_target_pairs={{0,8},{8,16},{16,24},{24,32},{32,40},{40,48},{48,56},{56,64},{64,7... | collective-permute-start | bytes 49160 | tf_op jit(solution)/shard_map/ppermute | solution.py:19
  17.4 0.7 copy-start.5
  24.4 11.3 %all-to-all-start = ((f32[8,2,32,128]{3,2,1,0:T(8,128)}), f32[8,2,32,128]{3,2,1,0:T(8,128)S(1)}, u32[]{:S(2)}, u32[]{:S(2)}) async-start(f32[8,2,32,128]{3,2,1,0:T(8,128)} %broadcast_in_dim.63), calls=%async_computation | async-start | bytes 524288 | tf_op jit(solution)/shard_map/all_to_all | solution.py:33
  35.7 1.4 copy-start.2
  35.7 1.4 copy-start.3
  35.7 1.4 copy-start.1
  37.0 0.7 copy-start.4
  62.4 8.0 %collective-permute-start.5 = (f32[32,1,128]{2,0,1:T(8,128)S(1)}, f32[32,1,128]{2,0,1:T(8,128)S(1)}, u32[]{:S(2)}, u32[]{:S(2)}) collective-permute-start(f32[32,1,128]{2,0,1:T(8,128)S(1)} %get-tuple-element.58), channel_id=1, source_target_pairs={{8,0},{16,8},{24,16},{32,24},{40,32},{48,40},{56,48},{64,56},{72,6... | collective-permute-start | bytes 49160 | tf_op jit(solution)/shard_map/ppermute | solution.py:20
  63.3 7.0 %collective-permute-start.4 = (f32[32,1,128]{2,0,1:T(8,128)S(1)}, f32[32,1,128]{2,0,1:T(8,128)S(1)}, u32[]{:S(2)}, u32[]{:S(2)}) collective-permute-start(f32[32,1,128]{2,0,1:T(8,128)S(1)} %get-tuple-element.59), channel_id=1, source_target_pairs={{0,8},{8,16},{16,24},{24,32},{32,40},{40,48},{48,56},{56,64},{64,7... | collective-permute-start | bytes 49160 | tf_op jit(solution)/shard_map/ppermute | solution.py:19
  63.9 20.5 %collective-permute-start.6 = (f32[1,16,128]{2,0,1:T(1,128)S(1)}, f32[1,16,128]{2,0,1:T(1,128)S(1)}, u32[]{:S(2)}, u32[]{:S(2)}) collective-permute-start(f32[1,16,128]{2,0,1:T(1,128)S(1)} %get-tuple-element.60), channel_id=1, source_target_pairs={{1,0},{2,1},{3,2},{4,3},{5,4},{6,5},{7,6},{9,8},{10,9},{11,10},{12... | collective-permute-start | bytes 24584 | tf_op jit(solution)/shard_map/ppermute | solution.py:20
  68.2 16.1 %collective-permute-start.7 = (f32[1,16,128]{2,0,1:T(1,128)S(1)}, f32[1,16,128]{2,0,1:T(1,128)S(1)}, u32[]{:S(2)}, u32[]{:S(2)}) collective-permute-start(f32[1,16,128]{2,0,1:T(1,128)S(1)} %get-tuple-element.61), channel_id=1, source_target_pairs={{0,1},{1,2},{2,3},{3,4},{4,5},{5,6},{6,7},{8,9},{9,10},{10,11},{11... | collective-permute-start | bytes 24584 | tf_op jit(solution)/shard_map/ppermute | solution.py:19
  71.1 12.0 %all-to-all-start.3 = ((f32[8,2,32,128]{3,2,1,0:T(8,128)}), f32[8,2,32,128]{3,2,1,0:T(8,128)S(1)}, u32[]{:S(2)}, u32[]{:S(2)}) async-start(f32[8,2,32,128]{3,2,1,0:T(8,128)} %broadcast_in_dim.68), calls=%async_computation.3 | async-start | bytes 524288 | tf_op jit(solution)/shard_map/all_to_all | solution.py:33
  115.3 8.3 %collective-permute-start.9 = (f32[32,1,128]{2,0,1:T(8,128)S(1)}, f32[32,1,128]{2,0,1:T(8,128)S(1)}, u32[]{:S(2)}, u32[]{:S(2)}) collective-permute-start(f32[32,1,128]{2,0,1:T(8,128)S(1)} %get-tuple-element.50), channel_id=1, source_target_pairs={{8,0},{16,8},{24,16},{32,24},{40,32},{48,40},{56,48},{64,56},{72,6... | collective-permute-start | bytes 49160 | tf_op jit(solution)/shard_map/ppermute | solution.py:20
  116.3 7.3 %collective-permute-start.8 = (f32[32,1,128]{2,0,1:T(8,128)S(1)}, f32[32,1,128]{2,0,1:T(8,128)S(1)}, u32[]{:S(2)}, u32[]{:S(2)}) collective-permute-start(f32[32,1,128]{2,0,1:T(8,128)S(1)} %get-tuple-element.51), channel_id=1, source_target_pairs={{0,8},{8,16},{16,24},{24,32},{32,40},{40,48},{48,56},{56,64},{64,7... | collective-permute-start | bytes 49160 | tf_op jit(solution)/shard_map/ppermute | solution.py:19
  116.8 20.7 %collective-permute-start.10 = (f32[1,16,128]{2,0,1:T(1,128)S(1)}, f32[1,16,128]{2,0,1:T(1,128)S(1)}, u32[]{:S(2)}, u32[]{:S(2)}) collective-permute-start(f32[1,16,128]{2,0,1:T(1,128)S(1)} %get-tuple-element.52), channel_id=1, source_target_pairs={{1,0},{2,1},{3,2},{4,3},{5,4},{6,5},{7,6},{9,8},{10,9},{11,10},{12... | collective-permute-start | bytes 24584 | tf_op jit(solution)/shard_map/ppermute | solution.py:20
  121.4 16.1 %collective-permute-start.11 = (f32[1,16,128]{2,0,1:T(1,128)S(1)}, f32[1,16,128]{2,0,1:T(1,128)S(1)}, u32[]{:S(2)}, u32[]{:S(2)}) collective-permute-start(f32[1,16,128]{2,0,1:T(1,128)S(1)} %get-tuple-element.53), channel_id=1, source_target_pairs={{0,1},{1,2},{2,3},{3,4},{4,5},{5,6},{6,7},{8,9},{9,10},{10,11},{11... | collective-permute-start | bytes 24584 | tf_op jit(solution)/shard_map/ppermute | solution.py:19
  124.3 12.0 %all-to-all-start.6 = ((f32[8,2,32,128]{3,2,1,0:T(8,128)}), f32[8,2,32,128]{3,2,1,0:T(8,128)S(1)}, u32[]{:S(2)}, u32[]{:S(2)}) async-start(f32[8,2,32,128]{3,2,1,0:T(8,128)} %broadcast_in_dim.73), calls=%async_computation.6 | async-start | bytes 524288 | tf_op jit(solution)/shard_map/all_to_all | solution.py:33
  181.7 12.5 %all-to-all-start.10 = ((f32[32,1,1]{2,1,0:T(1,128)}), f32[32,1,1]{2,1,0:T(1,128)S(1)}, u32[]{:S(2)}, u32[]{:S(2)}) async-start(f32[32,1,1]{2,1,0:T(1,128)} %broadcast_in_dim.79), calls=%async_computation.10 | async-start | bytes 32768 | tf_op jit(solution)/shard_map/all_to_all | solution.py:33
where the time goes:
time: 198 us; the launch traced here: 197 us
  blocking collectives  69.8 us (35%)
  starting transfers between devices  50.3 us (25%)
  waiting for transfers between devices  29.6 us (15%)
  local copies, waits for them, and re-layouts  21.5 us (11%)
  other arithmetic  14.3 us (7%)
  between operations  9.54 us (5%)
  matrix products  2.09 us (1%)
    all_to_all x7, blocking collectives, from_everyone(): return lax.all_to_all(copies, axis, split_axis=0, concat_axis=0, tiled=True)  69.8 us
    all_to_all x4, waiting for transfers between devices, from_everyone(): return lax.all_to_all(copies, axis, split_axis=0, concat_axis=0, tiled=True)  24.1 us
    ppermute x6, starting transfers between devices, padded(): after = lax.ppermute(initial, axis, down)  23.5 us
    all_to_all x4, starting transfers between devices, from_everyone(): return lax.all_to_all(copies, axis, split_axis=0, concat_axis=0, tiled=True)  19.6 us
    another operation x2, local copies, waits for them, and re-layouts, on_device(): jnp.stack(terms)  7.79 us
    ppermute x6, starting transfers between devices, padded(): before = lax.ppermute(last, axis, up)  7.21 us
    reduce_sum x4, other arithmetic, local_product(): return jnp.sum(left * right)  5.63 us
    ppermute x6, waiting for transfers between devices, padded(): before = lax.ppermute(last, axis, up)  5.38 us
  transfers between devices with their start and end apart: 16, of which 6 were waited for; matrix products, arithmetic and copies ran while one was open for 5% of the time, Pallas kernels for 0%

commit v1 on v0

v1 whole, which is shorter than its diff:
```python
import functools

import jax
import jax.numpy as jnp
from jax import lax
from jax.experimental import pallas as pl
from jax.experimental.pallas import tpu as pltpu
from jax.sharding import PartitionSpec as P

ITERS = 3
MESH = pl.DeviceIdType.MESH
F32 = jnp.float32
BF16 = jnp.bfloat16


def split(x):
    hi = x.astype(BF16)
    return hi, (x - hi.astype(F32)).astype(BF16)


def kernel(
    n_gx, n_gy, rows, cols,
    r_hbm, d_hbm, h_hbm, vert_ref, m_hbm, er_ref,
    x_hbm, res_hbm, sq_ref,
    r_v, d_v, h_v, m_v, w_hi, w_lo, z_v, u_v, t_v, x_v, o_v,
    send_e, send_w, send_n, send_s, hal_n, hal_s, ce0, ce1, ce2, cw0, cw1, cw2, gat_e, gat_w, part1, part2, recv1, recv2,
    ld_sem, ss_e, ss_w, ss_n, ss_s, rs_e, rs_w, rs_n, rs_s, ss_1, ss_2, rs_1, rs_2, st_sem,
):
    gx = lax.axis_index("gx")
    gy = lax.axis_index("gy")
    half = n_gx // 2
    cells = rows * cols
    total_cells = float(cells * 128 * n_gx * n_gy)
    lev = 128
    edge_e = jnp.logical_or(gx == half - 1, gx == n_gx - 1)
    edge_w = jnp.logical_or(gx == half, gx == 0)
    edge = jnp.logical_or(edge_e, edge_w)
    east = lax.rem(gx + 1, n_gx)
    west = lax.rem(gx + n_gx - 1, n_gx)
    across = jnp.where(edge_e, east, west)
    panel = (gx >= half).astype(jnp.int32)
    pad = 8
    col_e = (ce0, ce1, ce2)
    col_w = (cw0, cw1, cw2)

    loads = [
        pltpu.make_async_copy(m_hbm.at[panel], m_v, ld_sem.at[0]),
        pltpu.make_async_copy(r_hbm, r_v, ld_sem.at[1]),
        pltpu.make_async_copy(d_hbm, d_v, ld_sem.at[2]),
        pltpu.make_async_copy(h_hbm, h_v, ld_sem.at[3]),
    ]
    for c in loads:
        c.start()

    barrier = pltpu.get_barrier_semaphore()
    for i in range(1, n_gx):
        pl.semaphore_signal(barrier, inc=1, device_id=(lax.rem(gx + i, n_gx), gy), device_id_type=MESH)
    for i in range(1, n_gy):
        pl.semaphore_signal(barrier, inc=1, device_id=(gx, lax.rem(gy + i, n_gy)), device_id_type=MESH)

    @pl.when(edge)
    def _():
        for i in range(1, n_gy):
            pl.semaphore_signal(barrier, inc=1, device_id=(across, lax.rem(gy + i, n_gy)), device_id_type=MESH)

    loads[0].wait()
    mt = m_v[...].T
    lane = lax.broadcasted_iota(jnp.int32, (lev, lev), 1)
    nxt = jnp.where(lane == lev - 1, 0.0, pltpu.roll(mt, lev - 1, 1))
    prv = jnp.where(lane == 0, 0.0, pltpu.roll(mt, 1, 1))
    vt = vert_ref[...] * (2.0 * mt - nxt - prv)
    for block, value in ((0, mt), (1, vt)):
        hi, lo = split(value)
        for half_k in range(2):
            w_hi[lev * half_k : lev * (half_k + 1), lev * block : lev * (block + 1)] = hi
            w_lo[lev * half_k : lev * (half_k + 1), lev * block : lev * (block + 1)] = lo

    def times(x, width):
        a, b = split(x)
        lhs = jnp.concatenate([a, b], 1)
        return jnp.dot(lhs, w_lo[:, :width], preferred_element_type=F32) + jnp.dot(
            lhs, w_hi[:, :width], preferred_element_type=F32
        )

    for k in range(ITERS):
        z_v[k, 0:pad, :] = jnp.zeros((pad, lev), F32)
        z_v[k, pad + cells :, :] = jnp.zeros((pad, lev), F32)

    @pl.when(gy == 0)
    def _():
        hal_s[...] = jnp.zeros_like(hal_s)

    @pl.when(gy == n_gy - 1)
    def _():
        hal_n[...] = jnp.zeros_like(hal_n)

    loads[1].wait()

    first = pl.ds(0, rows, stride=cols)
    last = pl.ds(cols - 1, rows, stride=cols)
    grams = {}

    def accumulate(i, j):
        a, b = field(i), field(j)
        grams[(i, j)] = jnp.sum((a * b).reshape(cells // 8, 8, lev), 0)

    def field(i):
        return r_v[...] if i == 0 else u_v[i - 1]

    for step in range(ITERS):
        src = r_v if step == 0 else u_v.at[step - 1]
        edge_rows_in = jnp.concatenate(
            [src[last, :], src[first, :], src[cells - cols :, :], src[0:cols, :]], 0
        )
        bnd = times(edge_rows_in, lev)
        send_e[step] = bnd[0:rows]
        send_w[step] = bnd[rows : 2 * rows]
        send_n[step] = bnd[2 * rows : 2 * rows + cols]
        send_s[step] = bnd[2 * rows + cols :]

        if step == 0:
            @pl.when(edge)
            def _():
                pl.semaphore_wait(barrier, n_gx - 1 + 2 * (n_gy - 1))

            @pl.when(jnp.logical_not(edge))
            def _():
                pl.semaphore_wait(barrier, n_gx - 1 + n_gy - 1)

        def side(is_edge, send, col, ss, rs, target):
            def copy(dst_gy, slot, i):
                return pltpu.make_async_remote_copy(
                    src_ref=send.at[step],
                    dst_ref=col[step].at[pl.ds(pl.multiple_of(slot * rows, rows), rows)],
                    send_sem=ss.at[step],
                    recv_sem=rs.at[step],
                    device_id=(target, dst_gy),
                    device_id_type=MESH,
                )

            @pl.when(is_edge)
            def _():
                for i in range(n_gy):
                    copy(lax.rem(gy + i + n_gy // 2, n_gy), gy, i).start()

            @pl.when(jnp.logical_not(is_edge))
            def _():
                copy(gy, 0, 0).start()

        side(edge_e, send_e, col_w, ss_e, rs_w, east)
        side(edge_w, send_w, col_e, ss_w, rs_e, west)
        north = pltpu.make_async_remote_copy(
            src_ref=send_n.at[step], dst_ref=hal_s.at[step],
            send_sem=ss_n.at[step], recv_sem=rs_s.at[step],
            device_id=(gx, lax.rem(gy + 1, n_gy)), device_id_type=MESH,
        )
        south = pltpu.make_async_remote_copy(
            src_ref=send_s.at[step], dst_ref=hal_n.at[step],
            send_sem=ss_s.at[step], recv_sem=rs_n.at[step],
            device_id=(gx, lax.rem(gy + n_gy - 1, n_gy)), device_id_type=MESH,
        )

        @pl.when(gy < n_gy - 1)
        def _():
            north.start()

        @pl.when(gy > 0)
        def _():
            south.start()

        both = times(src[...], 2 * lev)
        z_v[step, pad : pad + cells, :] = both[:, :lev]
        t_v[...] = both[:, lev:]
        if step == 0:
            loads[2].wait()
            loads[3].wait()
        row = lax.broadcasted_iota(jnp.int32, (cols, lev), 0)
        for y in range(rows):
            here = pl.ds(pad + y * cols, cols)
            z = z_v[step, here, :]
            e = jnp.where(row == cols - 1, 0.0, z_v[step, pl.ds(pad + y * cols + 1, cols), :])
            w = jnp.where(row == 0, 0.0, z_v[step, pl.ds(pad + y * cols - 1, cols), :])
            beside = e + w
            if y < rows - 1:
                beside = beside + z_v[step, pl.ds(pad + (y + 1) * cols, cols), :]
            if y > 0:
                beside = beside + z_v[step, pl.ds(pad + (y - 1) * cols, cols), :]
            at = pl.ds(y * cols, cols)
            u_v[step, at, :] = d_v[at, :] * z + h_v[at, :] * (4.0 * z - beside) + t_v[at, :]

        for j in range(step + 1):
            accumulate(j, step)

        @pl.when(gy < n_gy - 1)
        def _():
            south.wait_recv()

        @pl.when(gy > 0)
        def _():
            north.wait_recv()

        tail = pl.ds(cells - cols, cols)
        u_v[step, tail, :] = u_v[step, tail, :] - h_v[tail, :] * hal_n[step]
        head = pl.ds(0, cols)
        u_v[step, head, :] = u_v[step, head, :] - h_v[head, :] * hal_s[step]

        def land(is_edge, col, rs, gat, which):
            @pl.when(is_edge)
            def _():
                pltpu.make_async_copy(col[step], col[step], rs.at[step]).wait()
                for y in range(rows):
                    gat[step, y : y + 1, :] = col[step][pl.ds(er_ref[which, gy * rows + y], 1), :]

            @pl.when(jnp.logical_not(is_edge))
            def _():
                one = col[step].at[pl.ds(0, rows)]
                pltpu.make_async_copy(one, one, rs.at[step]).wait()
                gat[step] = col[step][0:rows, :]

        land(edge_e, col_e, rs_e, gat_e, jnp.where(gx == half - 1, 0, 1))
        land(edge_w, col_w, rs_w, gat_w, jnp.where(gx == half, 0, 1))
        u_v[step, last, :] = u_v[step, last, :] - h_v[last, :] * gat_e[step]
        u_v[step, first, :] = u_v[step, first, :] - h_v[first, :] * gat_w[step]

    for j in range(ITERS + 1):
        accumulate(j, ITERS)

    keys = [(i, j) for j in range(ITERS + 1) for i in range(j + 1)]
    stack = jnp.concatenate([jnp.sum(grams[key], 0, keepdims=True) for key in keys], 0)
    sums = jnp.sum(stack, 1, keepdims=True)
    n = len(keys)
    pick = lax.broadcasted_iota(jnp.int32, (n, lev), 0) == lax.broadcasted_iota(jnp.int32, (n, lev), 1)
    part1[...] = jnp.sum(jnp.where(pick, sums, 0.0), 0, keepdims=True).reshape(1, 1, lev)

    def share(part, recv, ss, rs, count, me, device):
        copies = []
        for i in range(1, count):
            peer = lax.rem(me + i, count)
            copies.append(
                pltpu.make_async_remote_copy(
                    src_ref=part, dst_ref=recv.at[pl.ds(count - 1 - i, 1)],
                    send_sem=ss, recv_sem=rs,
                    device_id=device(peer), device_id_type=MESH,
                )
            )
        for c in copies:
            c.start()
        pltpu.make_async_copy(recv, recv, rs).wait()
        return part[...] + jnp.sum(recv[...], 0, keepdims=True)

    part2[...] = share(part1, recv1, ss_1, rs_1, n_gy, gy, lambda p: (gx, p))
    total = share(part2, recv2, ss_2, rs_2, n_gx, gx, lambda p: (p, gy))
    total = total.reshape(1, lev) * (1.0 / total_cells)
    lane1 = lax.broadcasted_iota(jnp.int32, (1, lev), 1)
    g = {}
    for number, key in enumerate(keys):
        g[key] = jnp.sum(jnp.where(lane1 == number, total, 0.0), 1, keepdims=True)

    s1 = 1.0 / jnp.sqrt(g[1, 1])
    a0 = g[0, 1] * s1
    l21 = g[1, 2] * s1
    l31 = g[1, 3] * s1
    s2 = 1.0 / jnp.sqrt(g[2, 2] - l21 * l21)
    a1 = (g[0, 2] - l21 * a0) * s2
    l32 = (g[2, 3] - l21 * l31) * s2
    s3 = 1.0 / jnp.sqrt(g[3, 3] - l31 * l31 - l32 * l32)
    a2 = (g[0, 3] - l31 * a0 - l32 * a1) * s3
    c3 = a2 * s3
    c2 = (a1 - l32 * c3) * s2
    c1 = (a0 - l21 * c2 - l31 * c3) * s1
    q0 = g[0, 0] - a0 * a0
    q1 = q0 - a1 * a1
    q2 = q1 - a2 * a2
    sq_ref[...] = jnp.where(lane1 == 0, q0, jnp.where(lane1 == 1, q1, q2))

    x_v[...] = c1 * z_v[0, pad : pad + cells, :] + c2 * z_v[1, pad : pad + cells, :] + c3 * z_v[2, pad : pad + cells, :]
    put_x = pltpu.make_async_copy(x_v, x_hbm, st_sem.at[0])
    put_x.start()
    o_v[...] = r_v[...] - c1 * u_v[0] - c2 * u_v[1] - c3 * u_v[2]
    put_o = pltpu.make_async_copy(o_v, res_hbm, st_sem.at[1])
    put_o.start()

    for step in range(ITERS):
        for is_edge, send, ss, col in ((edge_e, send_e, ss_e, col_e), (edge_w, send_w, ss_w, col_w)):
            @pl.when(is_edge)
            def _():
                pltpu.make_async_copy(col[step], col[step], ss.at[step]).wait()

            @pl.when(jnp.logical_not(is_edge))
            def _():
                pltpu.make_async_copy(send.at[step], send.at[step], ss.at[step]).wait()

        @pl.when(gy < n_gy - 1)
        def _():
            pltpu.make_async_copy(send_n.at[step], send_n.at[step], ss_n.at[step]).wait()

        @pl.when(gy > 0)
        def _():
            pltpu.make_async_copy(send_s.at[step], send_s.at[step], ss_s.at[step]).wait()

    pltpu.make_async_copy(recv1, recv1, ss_1).wait()
    pltpu.make_async_copy(recv2, recv2, ss_2).wait()
    put_x.wait()
    put_o.wait()


def on_device(n_gx, n_gy, right_side, diagonal, horizontal, vertical, precond, edge_rows):
    rows, cols, lev = right_side.shape
    cells = rows * cols
    flat = lambda a: a.reshape(cells, lev)
    hbm = pl.BlockSpec(memory_space=pl.ANY)
    vmem = pl.BlockSpec(memory_space=pltpu.VMEM)
    smem = pl.BlockSpec(memory_space=pltpu.SMEM)
    dma = pltpu.SemaphoreType.DMA
    scratch = [
        pltpu.VMEM((cells, lev), F32),
        pltpu.VMEM((cells, lev), F32),
        pltpu.VMEM((cells, lev), F32),
        pltpu.VMEM((lev, lev), F32),
        pltpu.VMEM((2 * lev, 2 * lev), BF16),
        pltpu.VMEM((2 * lev, 2 * lev), BF16),
        pltpu.VMEM((ITERS, cells + 16, lev), F32),
        pltpu.VMEM((ITERS, cells, lev), F32),
        pltpu.VMEM((cells, lev), F32),
        pltpu.VMEM((cells, lev), F32),
        pltpu.VMEM((cells, lev), F32),
        pltpu.VMEM((ITERS, rows, lev), F32),
        pltpu.VMEM((ITERS, rows, lev), F32),
        pltpu.VMEM((ITERS, cols, lev), F32),
        pltpu.VMEM((ITERS, cols, lev), F32),
        pltpu.VMEM((ITERS, cols, lev), F32),
        pltpu.VMEM((ITERS, cols, lev), F32),
        *[pltpu.VMEM((n_gy * rows, lev), F32)] * (2 * ITERS),
        pltpu.VMEM((ITERS, rows, lev), F32),
        pltpu.VMEM((ITERS, rows, lev), F32),
        pltpu.VMEM((1, 1, lev), F32),
        pltpu.VMEM((1, 1, lev), F32),
        pltpu.VMEM((n_gy - 1, 1, lev), F32),
        pltpu.VMEM((n_gx - 1, 1, lev), F32),
        dma((4,)),
        dma((ITERS,)), dma((ITERS,)), dma((ITERS,)), dma((ITERS,)),
        dma((ITERS,)), dma((ITERS,)), dma((ITERS,)), dma((ITERS,)),
        dma, dma, dma, dma,
        dma((2,)),
    ]
    x, res, sq = pl.pallas_call(
        functools.partial(kernel, n_gx, n_gy, rows, cols),
        out_shape=(
            jax.ShapeDtypeStruct((cells, lev), F32),
            jax.ShapeDtypeStruct((cells, lev), F32),
            jax.ShapeDtypeStruct((1, lev), F32),
        ),
        in_specs=[hbm, hbm, hbm, vmem, hbm, smem],
        out_specs=(hbm, hbm, vmem),
        scratch_shapes=scratch,
        compiler_params=pltpu.CompilerParams(collective_id=0, has_side_effects=True),
        name="solve",
    )(flat(right_side), flat(diagonal), flat(horizontal), vertical.reshape(1, lev), precond, edge_rows)
    return x.reshape(rows, cols, lev), res.reshape(rows, cols, lev), sq[0, :ITERS]


def solution(mesh):
    field = P("gy", "gx", None)
    return jax.shard_map(
        functools.partial(on_device, mesh.shape["gx"], mesh.shape["gy"]),
        mesh=mesh,
        in_specs=(field, field, field, P(), P(), P()),
        out_specs=(field, field, P()),
        check_vma=False,
    )
```

time: 198 us -> 47.9 us (0.24)
  blocking collectives: 69.8 us -> 0 us
  starting transfers between devices: 50.3 us -> 0 us
  Pallas kernels: 0 us -> 43.5 us
  waiting for transfers between devices: 29.6 us -> 0 us
  local copies, waits for them, and re-layouts: 21.5 us -> 3.56 us
  other arithmetic: 14.3 us -> 0 us
  between operations: 9.54 us -> 0.65 us
  matrix products: 2.09 us -> 0 us
    all_to_all x7 -> x0, blocking collectives: 69.8 us -> none  [from_everyone(): return lax.all_to_all(copies, axis, split_axis=0, concat_axis=0, tiled=True)]
    pallas_call x0 -> x1, Pallas kernels: none -> 43.5 us  [on_device(): pl.pallas_call(functools.partial(kernel, n_gx, n_gy, rows, cols), out_sha...]
    ppermute x12 -> x0, starting transfers between devices: 30.7 us -> none  [the longest x6 23.5 us: padded(): after = lax.ppermute(initial, axis, down)]
    all_to_all x4 -> x0, waiting for transfers between devices: 24.1 us -> none  [from_everyone(): return lax.all_to_all(copies, axis, split_axis=0, concat_axis=0, tiled=True)]
    all_to_all x4 -> x0, starting transfers between devices: 19.6 us -> none  [from_everyone(): return lax.all_to_all(copies, axis, split_axis=0, concat_axis=0, tiled=True)]
    reduce_sum x13 -> x0, other arithmetic: 7.87 us -> none  [the longest x4 5.63 us: local_product(): return jnp.sum(left * right)]
    another operation x2 -> x0, local copies, waits for them, and re-layouts: 7.79 us -> none  [on_device(): jnp.stack(terms)]
    ppermute x12 -> x0, waiting for transfers between devices: 5.45 us -> none  [the longest x6 5.38 us: padded(): before = lax.ppermute(last, axis, up)]
  transfers between devices with their start and end apart: 16 -> 0, of which waited for: 6 -> 0; matrix products, arithmetic and copies ran while one was open for 5% -> 0% of each run, Pallas kernels for 0% -> 0%
where the time goes in v1:
time: 47.9 us; the launch traced here: 47.7 us
  Pallas kernels  43.5 us (91%)
  local copies, waits for them, and re-layouts  3.56 us (7%)
  between operations  0.65 us (1%)
    pallas_call x1, Pallas kernels, on_device(): pl.pallas_call(functools.partial(kernel, n_gx, n_gy, rows, cols), out_sha...  43.5 us
    unnamed x6, local copies, waits for them, and re-layouts  3.04 us

profile of v1, /device:TPU:1, one launch (start us, length us, event | category | flops | bytes accessed | tf_op | source)
XLA Modules:
  0.0 47.7 jit_solution(17271800912146270306)
XLA Ops:
  0.6 43.5 %solve.1 = (f32[512,128]{1,0:T(8,128)}, f32[512,128]{1,0:T(8,128)}, f32[1,128]{1,0:T(1,128)}) custom-call(f32[512,128]{1,0:T(8,128)} %bitcast.8, f32[512,128]{1,0:T(8,128)} %bitcast.9, f32[512,128]{1,0:T(8,128)} %bitcast.10, f32[1,128]{1,0:T(1,128)} %bitcast.13, f32[2,128,128]{2,1,0:T(8,128)} %m_hbm.1, s32[2,256]{1,0:T(2,128)} %er_ref.1), custom_call_target="tpu_custom_call" | custom-call | tf_op jit(solution)/shard_map/solve/pallas_call | solution.py:346
  44.2 0.0 copy-start.1
  44.2 0.6 %copy-done.1 = f32[1,128]{1,0:T(1,128)S(1)} copy-done((f32[1,128]{1,0:T(1,128)S(1)}, f32[1,128]{1,0:T(1,128)}, u32[]{:S(2)}) %copy-start.1) | copy-done | bytes 536
  44.8 0.5 %slice_bitcast_fusion = f32[3]{0:T(128)} fusion(f32[1,128]{1,0:T(1,128)S(1)} %copy-done.1), kind=kLoop, calls=%fused_computation | loop fusion | bytes 24 | tf_op jit(solution)/shard_map/squeeze | solution.py:359
  45.3 0.0 copy-start
  45.3 1.7 %copy.11 = f32[32,16,128]{2,1,0:T(8,128)} copy(f32[32,16,128]{2,1,0:T(8,128)} %bitcast.12) | data formatting | bytes 524288
  47.0 0.0 copy-done
  47.0 0.7 %copy.12 = f32[32,16,128]{2,1,0:T(8,128)} copy(f32[32,16,128]{2,1,0:T(8,128)S(1)} %bitcast.11) | data formatting | bytes 524288
Async XLA Ops:
  44.2 0.6 %copy-start.1 = (f32[1,128]{1,0:T(1,128)S(1)}, f32[1,128]{1,0:T(1,128)}, u32[]{:S(2)}) copy-start(f32[1,128]{1,0:T(1,128)} %get-tuple-element.8) | copy-start | bytes 1540
  45.3 1.7 %copy-start = (f32[512,128]{1,0:T(8,128)S(1)}, f32[512,128]{1,0:T(8,128)}, u32[]{:S(2)}) copy-start(f32[512,128]{1,0:T(8,128)} %get-tuple-element.7) | copy-start | bytes 786436

commit v2 on v1

--- a/solution.py
+++ b/solution.py
@@ -20,11 +20,11 @@
 
 def kernel(
     n_gx, n_gy, rows, cols,
-    r_hbm, d_hbm, h_hbm, vert_ref, m_hbm, er_ref,
-    x_hbm, res_hbm, sq_ref,
-    r_v, d_v, h_v, m_v, w_hi, w_lo, z_v, u_v, t_v, x_v, o_v,
+    r_hbm, d_hbm, h_hbm, vert_hbm, m_hbm, er_hbm,
+    x_v, o_v, sq_ref,
+    r_v, d_v, h_v, vert_ref, m_v, er_ref, w_hi, w_lo, z_v, u_v, t_v,
     send_e, send_w, send_n, send_s, hal_n, hal_s, ce0, ce1, ce2, cw0, cw1, cw2, gat_e, gat_w, part1, part2, recv1, recv2,
-    ld_sem, ss_e, ss_w, ss_n, ss_s, rs_e, rs_w, rs_n, rs_s, ss_1, ss_2, rs_1, rs_2, st_sem,
+    ld_sem, ss_e, ss_w, ss_n, ss_s, rs_e, rs_w, rs_n, rs_s, ss_1, ss_2, rs_1, rs_2,
 ):
     gx = lax.axis_index("gx")
     gy = lax.axis_index("gy")
@@ -48,6 +48,8 @@
         pltpu.make_async_copy(r_hbm, r_v, ld_sem.at[1]),
         pltpu.make_async_copy(d_hbm, d_v, ld_sem.at[2]),
         pltpu.make_async_copy(h_hbm, h_v, ld_sem.at[3]),
+        pltpu.make_async_copy(vert_hbm, vert_ref, ld_sem.at[4]),
+        pltpu.make_async_copy(er_hbm, er_ref, ld_sem.at[5]),
     ]
     for c in loads:
         c.start()
@@ -64,6 +66,7 @@
             pl.semaphore_signal(barrier, inc=1, device_id=(across, lax.rem(gy + i, n_gy)), device_id_type=MESH)
 
     loads[0].wait()
+    loads[4].wait()
     mt = m_v[...].T
     lane = lax.broadcasted_iota(jnp.int32, (lev, lev), 1)
     nxt = jnp.where(lane == lev - 1, 0.0, pltpu.roll(mt, lev - 1, 1))
@@ -138,10 +141,16 @@
                     device_id_type=MESH,
                 )
 
+            def peer(i):
+                x, core = gy // 2, lax.rem(gy, 2)
+                chips = n_gy // 2
+                order = sorted(range(chips), key=lambda k: -min(k, chips - k))
+                return 2 * lax.rem(x + order[i // 2], chips) + lax.rem(core + i, 2)
+
             @pl.when(is_edge)
             def _():
                 for i in range(n_gy):
-                    copy(lax.rem(gy + i + n_gy // 2, n_gy), gy, i).start()
+                    copy(peer(i), gy, i).start()
 
             @pl.when(jnp.logical_not(is_edge))
             def _():
@@ -174,6 +183,7 @@
         if step == 0:
             loads[2].wait()
             loads[3].wait()
+            loads[5].wait()
         row = lax.broadcasted_iota(jnp.int32, (cols, lev), 0)
         for y in range(rows):
             here = pl.ds(pad + y * cols, cols)
@@ -274,11 +284,7 @@
     sq_ref[...] = jnp.where(lane1 == 0, q0, jnp.where(lane1 == 1, q1, q2))
 
     x_v[...] = c1 * z_v[0, pad : pad + cells, :] + c2 * z_v[1, pad : pad + cells, :] + c3 * z_v[2, pad : pad + cells, :]
-    put_x = pltpu.make_async_copy(x_v, x_hbm, st_sem.at[0])
-    put_x.start()
     o_v[...] = r_v[...] - c1 * u_v[0] - c2 * u_v[1] - c3 * u_v[2]
-    put_o = pltpu.make_async_copy(o_v, res_hbm, st_sem.at[1])
-    put_o.start()
 
     for step in range(ITERS):
         for is_edge, send, ss, col in ((edge_e, send_e, ss_e, col_e), (edge_w, send_w, ss_w, col_w)):
@@ -300,8 +306,20 @@
 
     pltpu.make_async_copy(recv1, recv1, ss_1).wait()
     pltpu.make_async_copy(recv2, recv2, ss_2).wait()
-    put_x.wait()
-    put_o.wait()
+
+
+def write_out(x_v, o_v, sq_v, x_hbm, res_hbm, sq_hbm, sq_s, sem):
+    copies = [pltpu.make_async_copy(x_v, x_hbm, sem.at[0]), pltpu.make_async_copy(o_v, res_hbm, sem.at[1])]
+    for c in copies:
+        c.start()
+    row = sq_v[...]
+    for i in range(ITERS):
+        sq_s[i] = row[0, i]
+    last = pltpu.make_async_copy(sq_s, sq_hbm, sem.at[2])
+    last.start()
+    for c in copies:
+        c.wait()
+    last.wait()
 
 
 def on_device(n_gx, n_gy, right_side, diagonal, horizontal, vertical, precond, edge_rows):
@@ -316,13 +334,13 @@
         pltpu.VMEM((cells, lev), F32),
         pltpu.VMEM((cells, lev), F32),
         pltpu.VMEM((cells, lev), F32),
+        pltpu.VMEM((1, lev), F32),
         pltpu.VMEM((lev, lev), F32),
+        pltpu.SMEM((2, n_gy * rows), jnp.int32),
         pltpu.VMEM((2 * lev, 2 * lev), BF16),
         pltpu.VMEM((2 * lev, 2 * lev), BF16),
         pltpu.VMEM((ITERS, cells + 16, lev), F32),
         pltpu.VMEM((ITERS, cells, lev), F32),
-        pltpu.VMEM((cells, lev), F32),
-        pltpu.VMEM((cells, lev), F32),
         pltpu.VMEM((cells, lev), F32),
         pltpu.VMEM((ITERS, rows, lev), F32),
         pltpu.VMEM((ITERS, rows, lev), F32),
@@ -337,26 +355,37 @@
         pltpu.VMEM((1, 1, lev), F32),
         pltpu.VMEM((n_gy - 1, 1, lev), F32),
         pltpu.VMEM((n_gx - 1, 1, lev), F32),
-        dma((4,)),
+        dma((6,)),
         dma((ITERS,)), dma((ITERS,)), dma((ITERS,)), dma((ITERS,)),
         dma((ITERS,)), dma((ITERS,)), dma((ITERS,)), dma((ITERS,)),
         dma, dma, dma, dma,
-        dma((2,)),
     ]
     x, res, sq = pl.pallas_call(
         functools.partial(kernel, n_gx, n_gy, rows, cols),
         out_shape=(
-            jax.ShapeDtypeStruct((cells, lev), F32),
-            jax.ShapeDtypeStruct((cells, lev), F32),
-            jax.ShapeDtypeStruct((1, lev), F32),
+            pltpu.VMEM((cells, lev), F32),
+            pltpu.VMEM((cells, lev), F32),
+            pltpu.VMEM((1, lev), F32),
         ),
-        in_specs=[hbm, hbm, hbm, vmem, hbm, smem],
-        out_specs=(hbm, hbm, vmem),
+        in_specs=[hbm, hbm, hbm, hbm, hbm, hbm],
+        out_specs=(vmem, vmem, vmem),
         scratch_shapes=scratch,
         compiler_params=pltpu.CompilerParams(collective_id=0, has_side_effects=True),
         name="solve",
     )(flat(right_side), flat(diagonal), flat(horizontal), vertical.reshape(1, lev), precond, edge_rows)
-    return x.reshape(rows, cols, lev), res.reshape(rows, cols, lev), sq[0, :ITERS]
+    x, res, sq = pl.pallas_call(
+        write_out,
+        out_shape=(
+            jax.ShapeDtypeStruct((cells, lev), F32),
+            jax.ShapeDtypeStruct((cells, lev), F32),
+            jax.ShapeDtypeStruct((ITERS,), F32),
+        ),
+        in_specs=[vmem, vmem, vmem],
+        out_specs=(hbm, hbm, hbm),
+        scratch_shapes=[pltpu.SMEM((ITERS,), F32), dma((3,))],
+        name="put",
+    )(*[pltpu.with_memory_space_constraint(a, pltpu.VMEM) for a in (x, res, sq)])
+    return x.reshape(rows, cols, lev), res.reshape(rows, cols, lev), sq
 
 
 def solution(mesh):

time: 47.9 us -> 43 us (0.90)
  local copies, waits for them, and re-layouts: 3.56 us -> 0 us
  Pallas kernels: 43.5 us -> 42.3 us
    unnamed x6 -> x0, local copies, waits for them, and re-layouts: 3.04 us -> none
    pallas_call x1, Pallas kernels: 43.5 us -> 41.5 us  [on_device(): pl.pallas_call(functools.partial(kernel, n_gx, n_gy, rows, cols), out_sha...]
    pallas_call x0 -> x1, Pallas kernels: none -> 0.83 us  [on_device(): pl.pallas_call(write_out, out_shape=(jax.ShapeDtypeStruct((cells, lev), F...]
    squeeze x1 -> x0, local copies, waits for them, and re-layouts: 0.51 us -> none  [on_device(): sq[0, :ITERS]]
where the time goes in v2:
time: 43 us; the launch traced here: 42.9 us
  Pallas kernels  42.3 us (98%)
  between operations  0.64 us (1%)
    pallas_call x1, Pallas kernels, on_device(): pl.pallas_call(functools.partial(kernel, n_gx, n_gy, rows, cols), out_sha...  41.5 us

profile of v2, /device:TPU:1, one launch (start us, length us, event | category | flops | bytes accessed | tf_op | source)
XLA Modules:
  0.0 42.9 jit_solution(7599250552193381430)
XLA Ops:
  0.6 41.5 %solve.1 = (f32[512,128]{1,0:T(8,128)S(1)}, f32[512,128]{1,0:T(8,128)S(1)}, f32[1,128]{1,0:T(1,128)S(1)}) custom-call(f32[512,128]{1,0:T(8,128)} %bitcast.6, f32[512,128]{1,0:T(8,128)} %bitcast.7, f32[512,128]{1,0:T(8,128)} %bitcast.8, f32[1,128]{1,0:T(1,128)} %bitcast.9, f32[2,128,128]{2,1,0:T(8,128)} %m_hbm.1, s32[2,256]{1,0:T(2,128)} %er_hbm.1), custom_call_target="tpu_custom_call" | custom-call | tf_op jit(solution)/shard_map/solve/pallas_call | solution.py:363
  42.1 0.8 %put.1 = (f32[512,128]{1,0:T(8,128)}, f32[512,128]{1,0:T(8,128)}, f32[3]{0:T(128)}) custom-call(f32[512,128]{1,0:T(8,128)S(1)} %get-tuple-element.9.x_v, f32[512,128]{1,0:T(8,128)S(1)} %get-tuple-element.10.o_v, f32[1,128]{1,0:T(1,128)S(1)} %get-tuple-element.11.sq_v), custom_call_target="tpu_custom_call" | custom-call | tf_op jit(solution)/shard_map/put/pallas_call | solution.py:376

commit v3 on v2

--- a/solution.py
+++ b/solution.py
@@ -22,9 +22,12 @@
     n_gx, n_gy, rows, cols,
     r_hbm, d_hbm, h_hbm, vert_hbm, m_hbm, er_hbm,
     x_v, o_v, sq_ref,
-    r_v, d_v, h_v, vert_ref, m_v, er_ref, w_hi, w_lo, z_v, u_v, t_v,
-    send_e, send_w, send_n, send_s, hal_n, hal_s, ce0, ce1, ce2, cw0, cw1, cw2, gat_e, gat_w, part1, part2, recv1, recv2,
-    ld_sem, ss_e, ss_w, ss_n, ss_s, rs_e, rs_w, rs_n, rs_s, ss_1, ss_2, rs_1, rs_2,
+    r_v, d_v, h_v, vert_ref, m_v, m2_v, er_v, w_hi, w_lo, w2_hi, w2_lo, z_v, u_v, t_v,
+    send_e, send_w, send_n, send_s, hal_e, hal_w, hal_n, hal_s,
+    pack_a, pack_z, own_a, opp_a, own_b, opp_b, opp_c, perm,
+    c1s_v, d2s_v, l2s_v, k1_v, d31_v, l31_v, d2o_v, l2o_v, k2s_v, d3s_v, l3s_v, d3o_v,
+    part1, part2, recv1, recv2,
+    ld_sem, ss_e, ss_w, ss_n, ss_s, rs_e, rs_w, rs_n, rs_s, ss_x, rs_x, fs_x, fr_x, ss_1, ss_2, rs_1, rs_2,
 ):
     gx = lax.axis_index("gx")
     gy = lax.axis_index("gy")
@@ -40,8 +43,18 @@
     across = jnp.where(edge_e, east, west)
     panel = (gx >= half).astype(jnp.int32)
     pad = 8
-    col_e = (ce0, ce1, ce2)
-    col_w = (cw0, cw1, cw2)
+    chips = n_gy // 2
+    chip, core = gy // 2, lax.rem(gy, 2)
+    full = n_gy * rows
+    at_e = edge_e.astype(jnp.int32)
+    x0 = at_e * (cols - 1)
+    x1 = x0 + 1 - 2 * at_e
+    x2 = x1 + 1 - 2 * at_e
+    table = jnp.logical_or(gx == 0, gx == n_gx - 1).astype(jnp.int32)
+
+    def column(x, base=0):
+        return pl.ds(base + x, rows, stride=cols)
+
 
     loads = [
         pltpu.make_async_copy(m_hbm.at[panel], m_v, ld_sem.at[0]),
@@ -49,7 +62,8 @@
         pltpu.make_async_copy(d_hbm, d_v, ld_sem.at[2]),
         pltpu.make_async_copy(h_hbm, h_v, ld_sem.at[3]),
         pltpu.make_async_copy(vert_hbm, vert_ref, ld_sem.at[4]),
-        pltpu.make_async_copy(er_hbm, er_ref, ld_sem.at[5]),
+        pltpu.make_async_copy(er_hbm, er_v, ld_sem.at[5]),
+        pltpu.make_async_copy(m_hbm.at[1 - panel], m2_v, ld_sem.at[6]),
     ]
     for c in loads:
         c.start()
@@ -65,30 +79,42 @@
         for i in range(1, n_gy):
             pl.semaphore_signal(barrier, inc=1, device_id=(across, lax.rem(gy + i, n_gy)), device_id_type=MESH)
 
+    def weights(m, hi_ref, lo_ref):
+        mt = m[...].T
+        lane = lax.broadcasted_iota(jnp.int32, (lev, lev), 1)
+        nxt = jnp.where(lane == lev - 1, 0.0, pltpu.roll(mt, lev - 1, 1))
+        prv = jnp.where(lane == 0, 0.0, pltpu.roll(mt, 1, 1))
+        vt = vert_ref[...] * (2.0 * mt - nxt - prv)
+        for block, value in ((0, mt), (1, vt)):
+            hi, lo = split(value)
+            for half_k in range(2):
+                hi_ref[lev * half_k : lev * (half_k + 1), lev * block : lev * (block + 1)] = hi
+                lo_ref[lev * half_k : lev * (half_k + 1), lev * block : lev * (block + 1)] = lo
+
     loads[0].wait()
     loads[4].wait()
-    mt = m_v[...].T
-    lane = lax.broadcasted_iota(jnp.int32, (lev, lev), 1)
-    nxt = jnp.where(lane == lev - 1, 0.0, pltpu.roll(mt, lev - 1, 1))
-    prv = jnp.where(lane == 0, 0.0, pltpu.roll(mt, 1, 1))
-    vt = vert_ref[...] * (2.0 * mt - nxt - prv)
-    for block, value in ((0, mt), (1, vt)):
-        hi, lo = split(value)
-        for half_k in range(2):
-            w_hi[lev * half_k : lev * (half_k + 1), lev * block : lev * (block + 1)] = hi
-            w_lo[lev * half_k : lev * (half_k + 1), lev * block : lev * (block + 1)] = lo
-
-    def times(x, width):
+    weights(m_v, w_hi, w_lo)
+
+    def times(x, width, other=False):
         a, b = split(x)
         lhs = jnp.concatenate([a, b], 1)
-        return jnp.dot(lhs, w_lo[:, :width], preferred_element_type=F32) + jnp.dot(
-            lhs, w_hi[:, :width], preferred_element_type=F32
+        hi, lo = (w2_hi, w2_lo) if other else (w_hi, w_lo)
+        return jnp.dot(lhs, lo[:, :width], preferred_element_type=F32) + jnp.dot(
+            lhs, hi[:, :width], preferred_element_type=F32
         )
 
     for k in range(ITERS):
         z_v[k, 0:pad, :] = jnp.zeros((pad, lev), F32)
         z_v[k, pad + cells :, :] = jnp.zeros((pad, lev), F32)
 
+    @pl.when(edge_e)
+    def _():
+        hal_e[...] = jnp.zeros_like(hal_e)
+
+    @pl.when(edge_w)
+    def _():
+        hal_w[...] = jnp.zeros_like(hal_w)
+
     @pl.when(gy == 0)
     def _():
         hal_s[...] = jnp.zeros_like(hal_s)
@@ -99,16 +125,49 @@
 
     loads[1].wait()
 
-    first = pl.ds(0, rows, stride=cols)
-    last = pl.ds(cols - 1, rows, stride=cols)
+    first = column(0)
+    last = column(cols - 1)
+
+    def remote(src, dst, send_sem, recv_sem, device):
+        return pltpu.make_async_remote_copy(
+            src_ref=src, dst_ref=dst, send_sem=send_sem, recv_sem=recv_sem, device_id=device, device_id_type=MESH
+        )
+
+    far_first = sorted(range(chips), key=lambda k: -min(k, chips - k))
+
+    def spread(number, pack_own, pack_opp, own, opp):
+        for k in far_first:
+            to = 2 * lax.rem(chip + k, chips) + core
+            remote(pack_opp, opp.at[:, chip, core], ss_x.at[number, 0], rs_x.at[number, 0], (across, to)).start()
+            if k:
+                remote(pack_own, own.at[:, chip, core], ss_x.at[number, 1], rs_x.at[number, 1], (gx, to)).start()
+
+    def arrived(ref, sem):
+        pltpu.make_async_copy(ref, ref, sem).wait()
+
+    def hand_over(number, own, opp):
+        sibling = (gx, gy + 1 - 2 * core)
+        for which, buf in ((0, opp), (1, own)):
+            arrived(buf.at[:, pl.ds(0, chips - which), core], rs_x.at[number, which])
+            remote(buf.at[:, :, core], buf.at[:, :, core], fs_x.at[number, which], fr_x.at[number, which], sibling).start()
+
+    def handed(number, own, opp):
+        for which, buf in ((0, opp), (1, own)):
+            arrived(buf.at[:, :, core], fr_x.at[number, which])
+
+    def sent(number, pack_own, pack_opp, own, opp):
+        arrived(opp.at[:, :, core], ss_x.at[number, 0])
+        arrived(own.at[:, pl.ds(0, chips - 1), core], ss_x.at[number, 1])
+        arrived(opp.at[:, :, core], fs_x.at[number, 0])
+        arrived(own.at[:, :, core], fs_x.at[number, 1])
+
     grams = {}
-
-    def accumulate(i, j):
-        a, b = field(i), field(j)
-        grams[(i, j)] = jnp.sum((a * b).reshape(cells // 8, 8, lev), 0)
 
     def field(i):
         return r_v[...] if i == 0 else u_v[i - 1]
+
+    def accumulate(i, j):
+        grams[(i, j)] = jnp.sum((field(i) * field(j)).reshape(cells // 8, 8, lev), 0)
 
     for step in range(ITERS):
         src = r_v if step == 0 else u_v.at[step - 1]
@@ -130,34 +189,38 @@
             def _():
                 pl.semaphore_wait(barrier, n_gx - 1 + n_gy - 1)
 
-        def side(is_edge, send, col, ss, rs, target):
-            def copy(dst_gy, slot, i):
-                return pltpu.make_async_remote_copy(
-                    src_ref=send.at[step],
-                    dst_ref=col[step].at[pl.ds(pl.multiple_of(slot * rows, rows), rows)],
-                    send_sem=ss.at[step],
-                    recv_sem=rs.at[step],
-                    device_id=(target, dst_gy),
-                    device_id_type=MESH,
-                )
-
-            def peer(i):
-                x, core = gy // 2, lax.rem(gy, 2)
-                chips = n_gy // 2
-                order = sorted(range(chips), key=lambda k: -min(k, chips - k))
-                return 2 * lax.rem(x + order[i // 2], chips) + lax.rem(core + i, 2)
-
-            @pl.when(is_edge)
-            def _():
-                for i in range(n_gy):
-                    copy(peer(i), gy, i).start()
-
-            @pl.when(jnp.logical_not(is_edge))
-            def _():
-                copy(gy, 0, 0).start()
-
-        side(edge_e, send_e, col_w, ss_e, rs_w, east)
-        side(edge_w, send_w, col_e, ss_w, rs_e, west)
+        @pl.when(edge)
+        def _():
+            mine = jnp.where(edge_e, bnd[0:rows], bnd[rows : 2 * rows])
+            if step == 0:
+                loads[2].wait()
+                loads[3].wait()
+                for q, value in enumerate((mine, h_v[column(x0), :], d_v[column(x0), :], h_v[column(x1), :])):
+                    pack_a[q] = value
+                    own_a[q, chip, core] = value
+                spread(0, pack_a, pack_a.at[pl.ds(0, 3)], own_a, opp_a)
+            elif step == 1:
+                pack_z[0] = mine
+                own_b[0, chip, core] = mine
+                spread(1, pack_z.at[pl.ds(0, 1)], pack_z.at[pl.ds(0, 1)], own_b, opp_b)
+            else:
+                pack_z[1] = mine
+                for k in far_first:
+                    for c in range(2):
+                        to = 2 * lax.rem(chip + k, chips) + c
+                        remote(pack_z.at[1], opp_c.at[chip, core], ss_x.at[2, 0], rs_x.at[2, 0], (across, to)).start()
+
+        to_east = remote(send_e.at[step], hal_w.at[step], ss_e.at[step], rs_w.at[step], (east, gy))
+        to_west = remote(send_w.at[step], hal_e.at[step], ss_w.at[step], rs_e.at[step], (west, gy))
+
+        @pl.when(jnp.logical_not(edge_e))
+        def _():
+            to_east.start()
+
+        @pl.when(jnp.logical_not(edge_w))
+        def _():
+            to_west.start()
+
         north = pltpu.make_async_remote_copy(
             src_ref=send_n.at[step], dst_ref=hal_s.at[step],
             send_sem=ss_n.at[step], recv_sem=rs_s.at[step],
@@ -181,9 +244,21 @@
         z_v[step, pad : pad + cells, :] = both[:, :lev]
         t_v[...] = both[:, lev:]
         if step == 0:
-            loads[2].wait()
-            loads[3].wait()
+            @pl.when(jnp.logical_not(edge))
+            def _():
+                loads[2].wait()
+                loads[3].wait()
+
             loads[5].wait()
+            loads[6].wait()
+
+            @pl.when(edge)
+            def _():
+                weights(m2_v, w2_hi, w2_lo)
+                row = er_v[pl.ds(table, 1), :]
+                hit = lax.broadcasted_iota(jnp.int32, (full, full), 0) == row
+                perm[...] = jnp.where(hit, 1.0, 0.0).T.astype(BF16)
+
         row = lax.broadcasted_iota(jnp.int32, (cols, lev), 0)
         for y in range(rows):
             here = pl.ds(pad + y * cols, cols)
@@ -198,8 +273,10 @@
             at = pl.ds(y * cols, cols)
             u_v[step, at, :] = d_v[at, :] * z + h_v[at, :] * (4.0 * z - beside) + t_v[at, :]
 
-        for j in range(step + 1):
-            accumulate(j, step)
+        if step == ITERS - 1:
+            @pl.when(edge)
+            def _():
+                hand_over(0, own_a, opp_a)
 
         @pl.when(gy < n_gy - 1)
         def _():
@@ -214,26 +291,89 @@
         head = pl.ds(0, cols)
         u_v[step, head, :] = u_v[step, head, :] - h_v[head, :] * hal_s[step]
 
-        def land(is_edge, col, rs, gat, which):
-            @pl.when(is_edge)
-            def _():
-                pltpu.make_async_copy(col[step], col[step], rs.at[step]).wait()
-                for y in range(rows):
-                    gat[step, y : y + 1, :] = col[step][pl.ds(er_ref[which, gy * rows + y], 1), :]
-
-            @pl.when(jnp.logical_not(is_edge))
-            def _():
-                one = col[step].at[pl.ds(0, rows)]
-                pltpu.make_async_copy(one, one, rs.at[step]).wait()
-                gat[step] = col[step][0:rows, :]
-
-        land(edge_e, col_e, rs_e, gat_e, jnp.where(gx == half - 1, 0, 1))
-        land(edge_w, col_w, rs_w, gat_w, jnp.where(gx == half, 0, 1))
-        u_v[step, last, :] = u_v[step, last, :] - h_v[last, :] * gat_e[step]
-        u_v[step, first, :] = u_v[step, first, :] - h_v[first, :] * gat_w[step]
-
-    for j in range(ITERS + 1):
-        accumulate(j, ITERS)
+        @pl.when(jnp.logical_not(edge_e))
+        def _():
+            to_west.wait_recv()
+
+        @pl.when(jnp.logical_not(edge_w))
+        def _():
+            to_east.wait_recv()
+
+        u_v[step, last, :] = u_v[step, last, :] - h_v[last, :] * hal_e[step]
+        u_v[step, first, :] = u_v[step, first, :] - h_v[first, :] * hal_w[step]
+
+    @pl.when(edge)
+    def _():
+        def whole(ref, *at):
+            return ref[at].reshape(full, lev) if at else ref[...].reshape(full, lev)
+
+        def met(x, which=None):
+            a, b = split(x)
+            matrix = perm[...] if which is None else perm[which, :]
+            out = jnp.dot(matrix, jnp.concatenate([a, b], 1), preferred_element_type=F32)
+            return out[:, :lev] + out[:, lev:]
+
+        line = lax.broadcasted_iota(jnp.int32, (full, lev), 0)
+
+        def along(x):
+            up = jnp.where(line == full - 1, 0.0, pltpu.roll(x, full - 1, 0))
+            return up + jnp.where(line == 0, 0.0, pltpu.roll(x, 1, 0))
+
+        def on_line(d, h, both):
+            x = both[:, :lev]
+            return (d + 4.0 * h) * x + both[:, lev:] - h * along(x)
+
+        handed(0, own_a, opp_a)
+        hs, ds, h1 = whole(own_a, 1), whole(own_a, 2), whole(own_a, 3)
+        ho, do = whole(opp_a, 1), whole(opp_a, 2)
+        c1s = -hs * met(whole(opp_a, 0))
+        c1s_v[...] = c1s
+        two = times(c1s, 2 * lev)
+        d2s = two[:, :lev]
+        d2s_v[...] = d2s
+        l2s_v[...] = on_line(ds, hs, two)
+        k1 = -h1 * d2s
+        k1_v[...] = k1
+        two = times(k1, 2 * lev)
+        d31_v[...] = two[:, :lev]
+        l31_v[...] = two[:, lev:]
+        c1o = -ho * met(whole(own_a, 0))
+        two = times(c1o, 2 * lev, True)
+        d2o_v[...] = two[:, :lev]
+        l2o_v[...] = on_line(do, ho, two)
+
+        hand_over(1, own_b, opp_b)
+        handed(1, own_b, opp_b)
+        hs, ho = whole(own_a, 1), whole(opp_a, 1)
+        k2s = l2s_v[...] - hs * met(whole(opp_b, 0) + d2o_v[...])
+        k2s_v[...] = k2s
+        k2o = l2o_v[...] - ho * met(whole(own_b, 0) + d2s_v[...])
+        d3o_v[...] = times(k2o, lev, True)
+        two = times(k2s, 2 * lev)
+        d3s_v[...] = two[:, :lev]
+        l3s_v[...] = on_line(whole(own_a, 2), hs, two)
+        l31_v[...] = l31_v[...] - whole(own_a, 3) * (along(d31_v[...]) + d3s_v[...])
+
+        here = pl.ds(pl.multiple_of(gy * rows, rows), rows)
+        c0, c1, c2 = column(x0), column(x1), column(x2)
+        p0, p1 = column(x0, pad), column(x1, pad)
+        d3s, d31 = d3s_v[here, :], d31_v[here, :]
+        h0, h_1 = h_v[c0, :], h_v[c1, :]
+        u_v[0, c0, :] = u_v[0, c0, :] + c1s_v[here, :]
+        u_v[1, c0, :] = u_v[1, c0, :] + k2s_v[here, :]
+        u_v[1, c1, :] = u_v[1, c1, :] + k1_v[here, :]
+        z_v[1, p0, :] = z_v[1, p0, :] + d2s_v[here, :]
+        z_v[2, p0, :] = z_v[2, p0, :] + d3s
+        z_v[2, p1, :] = z_v[2, p1, :] + d31
+        u_v[2, c1, :] = u_v[2, c1, :] + (d_v[c1, :] + 4.0 * h_1) * d31 + l31_v[here, :]
+        u_v[2, c2, :] = u_v[2, c2, :] - h_v[c2, :] * d31
+        partial = u_v[2, c0, :] + l3s_v[here, :] - h0 * d31
+        arrived(opp_c, rs_x.at[2, 0])
+        u_v[2, c0, :] = partial - h0 * met(whole(opp_c) + d3o_v[...], here)
+
+    for i in range(ITERS + 1):
+        for j in range(i, ITERS + 1):
+            accumulate(i, j)
 
     keys = [(i, j) for j in range(ITERS + 1) for i in range(j + 1)]
     stack = jnp.concatenate([jnp.sum(grams[key], 0, keepdims=True) for key in keys], 0)
@@ -287,14 +427,13 @@
     o_v[...] = r_v[...] - c1 * u_v[0] - c2 * u_v[1] - c3 * u_v[2]
 
     for step in range(ITERS):
-        for is_edge, send, ss, col in ((edge_e, send_e, ss_e, col_e), (edge_w, send_w, ss_w, col_w)):
-            @pl.when(is_edge)
-            def _():
-                pltpu.make_async_copy(col[step], col[step], ss.at[step]).wait()
-
-            @pl.when(jnp.logical_not(is_edge))
-            def _():
-                pltpu.make_async_copy(send.at[step], send.at[step], ss.at[step]).wait()
+        @pl.when(jnp.logical_not(edge_e))
+        def _():
+            arrived(send_e.at[step], ss_e.at[step])
+
+        @pl.when(jnp.logical_not(edge_w))
+        def _():
+            arrived(send_w.at[step], ss_w.at[step])
 
         @pl.when(gy < n_gy - 1)
         def _():
@@ -303,6 +442,12 @@
         @pl.when(gy > 0)
         def _():
             pltpu.make_async_copy(send_s.at[step], send_s.at[step], ss_s.at[step]).wait()
+
+    @pl.when(edge)
+    def _():
+        sent(0, pack_a, pack_a, own_a, opp_a)
+        sent(1, pack_z, pack_z, own_b, opp_b)
+        arrived(opp_c, ss_x.at[2, 0])
 
     pltpu.make_async_copy(recv1, recv1, ss_1).wait()
     pltpu.make_async_copy(recv2, recv2, ss_2).wait()
@@ -330,34 +475,38 @@
     vmem = pl.BlockSpec(memory_space=pltpu.VMEM)
     smem = pl.BlockSpec(memory_space=pltpu.SMEM)
     dma = pltpu.SemaphoreType.DMA
+    full = n_gy * rows
+    chips = n_gy // 2
     scratch = [
-        pltpu.VMEM((cells, lev), F32),
-        pltpu.VMEM((cells, lev), F32),
-        pltpu.VMEM((cells, lev), F32),
+        *[pltpu.VMEM((cells, lev), F32)] * 3,
         pltpu.VMEM((1, lev), F32),
-        pltpu.VMEM((lev, lev), F32),
-        pltpu.SMEM((2, n_gy * rows), jnp.int32),
-        pltpu.VMEM((2 * lev, 2 * lev), BF16),
-        pltpu.VMEM((2 * lev, 2 * lev), BF16),
+        *[pltpu.VMEM((lev, lev), F32)] * 2,
+        pltpu.VMEM((2, full), jnp.int32),
+        *[pltpu.VMEM((2 * lev, 2 * lev), BF16)] * 4,
         pltpu.VMEM((ITERS, cells + 16, lev), F32),
         pltpu.VMEM((ITERS, cells, lev), F32),
         pltpu.VMEM((cells, lev), F32),
-        pltpu.VMEM((ITERS, rows, lev), F32),
-        pltpu.VMEM((ITERS, rows, lev), F32),
-        pltpu.VMEM((ITERS, cols, lev), F32),
-        pltpu.VMEM((ITERS, cols, lev), F32),
-        pltpu.VMEM((ITERS, cols, lev), F32),
-        pltpu.VMEM((ITERS, cols, lev), F32),
-        *[pltpu.VMEM((n_gy * rows, lev), F32)] * (2 * ITERS),
-        pltpu.VMEM((ITERS, rows, lev), F32),
-        pltpu.VMEM((ITERS, rows, lev), F32),
+        *[pltpu.VMEM((ITERS, rows, lev), F32)] * 2,
+        *[pltpu.VMEM((ITERS, cols, lev), F32)] * 2,
+        *[pltpu.VMEM((ITERS, rows, lev), F32)] * 2,
+        *[pltpu.VMEM((ITERS, cols, lev), F32)] * 2,
+        pltpu.VMEM((4, rows, lev), F32),
+        pltpu.VMEM((2, rows, lev), F32),
+        pltpu.VMEM((4, chips, 2, rows, lev), F32),
+        pltpu.VMEM((3, chips, 2, rows, lev), F32),
+        pltpu.VMEM((1, chips, 2, rows, lev), F32),
+        pltpu.VMEM((1, chips, 2, rows, lev), F32),
+        pltpu.VMEM((chips, 2, rows, lev), F32),
+        pltpu.VMEM((full, full), BF16),
+        *[pltpu.VMEM((full, lev), F32)] * 12,
         pltpu.VMEM((1, 1, lev), F32),
         pltpu.VMEM((1, 1, lev), F32),
         pltpu.VMEM((n_gy - 1, 1, lev), F32),
         pltpu.VMEM((n_gx - 1, 1, lev), F32),
-        dma((6,)),
+        dma((7,)),
         dma((ITERS,)), dma((ITERS,)), dma((ITERS,)), dma((ITERS,)),
         dma((ITERS,)), dma((ITERS,)), dma((ITERS,)), dma((ITERS,)),
+        dma((3, 2)), dma((3, 2)), dma((2, 2)), dma((2, 2)),
         dma, dma, dma, dma,
     ]
     x, res, sq = pl.pallas_call(

time: 43 us -> 35.5 us (0.83)
  Pallas kernels: 42.3 us -> 34.7 us
    pallas_call x1, Pallas kernels: 41.5 us -> 33.9 us  [on_device(): pl.pallas_call(functools.partial(kernel, n_gx, n_gy, rows, cols), out_sha...]
where the time goes in v3:
time: 35.5 us; the launch traced here: 35.4 us
  Pallas kernels  34.7 us (98%)
  between operations  0.64 us (2%)
    pallas_call x1, Pallas kernels, on_device(): pl.pallas_call(functools.partial(kernel, n_gx, n_gy, rows, cols), out_sha...  33.9 us
    pallas_call x1, Pallas kernels, on_device(): pl.pallas_call(write_out, out_shape=(jax.ShapeDtypeStruct((cells, lev), F...  0.83 us

profile of v3, /device:TPU:1, one launch (start us, length us, event | category | flops | bytes accessed | tf_op | source)
XLA Modules:
  0.0 35.4 jit_solution(12879551520604346074)
XLA Ops:
  0.6 33.9 %solve.1 = (f32[512,128]{1,0:T(8,128)S(1)}, f32[512,128]{1,0:T(8,128)S(1)}, f32[1,128]{1,0:T(1,128)S(1)}) custom-call(f32[512,128]{1,0:T(8,128)} %bitcast.6, f32[512,128]{1,0:T(8,128)} %bitcast.7, f32[512,128]{1,0:T(8,128)} %bitcast.8, f32[1,128]{1,0:T(1,128)} %bitcast.9, f32[2,128,128]{2,1,0:T(8,128)} %m_hbm.1, s32[2,256]{1,0:T(2,128)} %er_hbm.1), custom_call_target="tpu_custom_call" | custom-call | tf_op jit(solution)/shard_map/solve/pallas_call | solution.py:512
  34.6 0.8 %put.1 = (f32[512,128]{1,0:T(8,128)}, f32[512,128]{1,0:T(8,128)}, f32[3]{0:T(128)}) custom-call(f32[512,128]{1,0:T(8,128)S(1)} %get-tuple-element.9.x_v, f32[512,128]{1,0:T(8,128)S(1)} %get-tuple-element.10.o_v, f32[1,128]{1,0:T(1,128)S(1)} %get-tuple-element.11.sq_v), custom_call_target="tpu_custom_call" | custom-call | tf_op jit(solution)/shard_map/put/pallas_call | solution.py:525

commit v4 on v3

--- a/solution.py
+++ b/solution.py
@@ -19,15 +19,15 @@
 
 
 def kernel(
-    n_gx, n_gy, rows, cols,
+    n_gx, n_gy, ny, rows, cols,
     r_hbm, d_hbm, h_hbm, vert_hbm, m_hbm, er_hbm,
     x_v, o_v, sq_ref,
     r_v, d_v, h_v, vert_ref, m_v, m2_v, er_v, w_hi, w_lo, w2_hi, w2_lo, z_v, u_v, t_v,
     send_e, send_w, send_n, send_s, hal_e, hal_w, hal_n, hal_s,
-    pack_a, pack_z, own_a, opp_a, own_b, opp_b, opp_c, perm,
-    c1s_v, d2s_v, l2s_v, k1_v, d31_v, l31_v, d2o_v, l2o_v, k2s_v, d3s_v, l3s_v, d3o_v,
+    pack_a, pack_b, pack_d, pack_g, own_a, opp_a, own_b, opp_b, own_d, opp_g, strip, perm, perm_w,
+    c1s_v, d2s_v, t2s_v, d2o_v, l2o_v,
     part1, part2, recv1, recv2,
-    ld_sem, ss_e, ss_w, ss_n, ss_s, rs_e, rs_w, rs_n, rs_s, ss_x, rs_x, fs_x, fr_x, ss_1, ss_2, rs_1, rs_2,
+    ld_sem, ss_e, ss_w, ss_n, ss_s, rs_e, rs_w, rs_n, rs_s, ss_x, rs_x, fs_x, fr_x, ss_t, rs_t, ss_d, rs_d, ss_g, rs_g, ss_1, ss_2, rs_1, rs_2,
 ):
     gx = lax.axis_index("gx")
     gy = lax.axis_index("gy")
@@ -68,16 +68,39 @@
     for c in loads:
         c.start()
 
+    plane = ny * n_gy
+    nz = n_gx // ny
+    z_, y_ = gx // ny, lax.rem(gx, ny)
+    in_plane = y_ * n_gy + gy
+
+    def at_plane(p):
+        return (z_ * ny + p // n_gy, lax.rem(p, n_gy))
+
+    def at_line(p):
+        return (p * ny + y_, gy)
+
     barrier = pltpu.get_barrier_semaphore()
-    for i in range(1, n_gx):
-        pl.semaphore_signal(barrier, inc=1, device_id=(lax.rem(gx + i, n_gx), gy), device_id_type=MESH)
-    for i in range(1, n_gy):
-        pl.semaphore_signal(barrier, inc=1, device_id=(gx, lax.rem(gy + i, n_gy)), device_id_type=MESH)
+
+    def greet(device):
+        pl.semaphore_signal(barrier, inc=1, device_id=device, device_id_type=MESH)
+
+    @pl.when(y_ == ny - 1)
+    def _():
+        greet((east, gy))
+
+    @pl.when(y_ == 0)
+    def _():
+        greet((west, gy))
 
     @pl.when(edge)
     def _():
         for i in range(1, n_gy):
-            pl.semaphore_signal(barrier, inc=1, device_id=(across, lax.rem(gy + i, n_gy)), device_id_type=MESH)
+            greet((across, lax.rem(gy + i, n_gy)))
+
+    for i in range(1, nz):
+        greet(at_line(lax.rem(z_ + i, nz)))
+    for i in range(1, plane):
+        greet(at_plane(lax.rem(in_plane + i, plane)))
 
     def weights(m, hi_ref, lo_ref):
         mt = m[...].T
@@ -107,6 +130,20 @@
         z_v[k, 0:pad, :] = jnp.zeros((pad, lev), F32)
         z_v[k, pad + cells :, :] = jnp.zeros((pad, lev), F32)
 
+    @pl.when(edge)
+    def _():
+        d2s_v[...] = jnp.zeros_like(d2s_v)
+        t2s_v[...] = jnp.zeros_like(t2s_v)
+        perm_w[...] = jnp.zeros_like(perm_w)
+
+        @pl.when(gy == 0)
+        def _():
+            strip[:, 0:8, :] = jnp.zeros((7, 8, lev), F32)
+
+        @pl.when(gy == n_gy - 1)
+        def _():
+            strip[:, 8 + rows :, :] = jnp.zeros((7, 8, lev), F32)
+
     @pl.when(edge_e)
     def _():
         hal_e[...] = jnp.zeros_like(hal_e)
@@ -168,6 +205,44 @@
 
     def accumulate(i, j):
         grams[(i, j)] = jnp.sum((field(i) * field(j)).reshape(cells // 8, 8, lev), 0)
+
+    strip_up = remote(
+        strip.at[:, pl.ds(rows, 8)], strip.at[:, pl.ds(0, 8)], ss_t.at[0], rs_t.at[0], (gx, lax.rem(gy + 1, n_gy))
+    )
+    strip_down = remote(
+        strip.at[:, pl.ds(8, 8)], strip.at[:, pl.ds(8 + rows, 8)], ss_t.at[1], rs_t.at[1],
+        (gx, lax.rem(gy + n_gy - 1, n_gy)),
+    )
+    block = pl.ds(pl.multiple_of(gy * rows, rows), rows)
+    near = pl.ds(pl.multiple_of(gy * rows, rows), rows + 16)
+    inner_rows = slice(8, 8 + rows)
+
+    def met(matrix, *xs):
+        out = jnp.dot(matrix, jnp.concatenate([p for x in xs for p in split(x)], 1), preferred_element_type=F32)
+        sums = [out[:, 2 * lev * n : 2 * lev * n + lev] + out[:, 2 * lev * n + lev : 2 * lev * (n + 1)] for n in range(len(xs))]
+        return sums[0] if len(xs) == 1 else sums
+
+    def window_along(x):
+        return pltpu.roll(x, 1, 0) + pltpu.roll(x, x.shape[0] - 1, 0)
+
+    def window_line(d, h, x, t):
+        return (d + 4.0 * h) * x + t - h * window_along(x)
+
+    def run_strip():
+        tall = rows + 16
+        two = times(jnp.concatenate([strip[0], strip[1], strip[2]], 0), 2 * lev)
+        za, zb, zc = [two[tall * n : tall * (n + 1), :lev] for n in range(3)]
+        ta, tb = [two[tall * n : tall * (n + 1), lev:] for n in range(2)]
+        ha, hb, da, db = strip[3], strip[4], strip[5], strip[6]
+        ua = window_line(da, ha, za, ta) - ha * zb
+        ub = window_line(db, hb, zb, tb) - hb * (za + zc)
+        two = times(jnp.concatenate([ua, ub], 0), 2 * lev)
+        z2a, z2b, t2a = two[:tall, :lev], two[tall:, :lev], two[:tall, lev:]
+        u2a = window_line(da, ha, z2a, t2a) - ha * z2b
+        z3a = times(u2a, lev)
+        pack_b[0] = z2a[inner_rows]
+        pack_b[1] = z3a[inner_rows]
+        own_b[0, chip, core] = z2a[inner_rows]
 
     for step in range(ITERS):
         src = r_v if step == 0 else u_v.at[step - 1]
@@ -181,34 +256,50 @@
         send_s[step] = bnd[2 * rows + cols :]
 
         if step == 0:
+            outer = jnp.logical_or(y_ == 0, y_ == ny - 1)
+
             @pl.when(edge)
             def _():
-                pl.semaphore_wait(barrier, n_gx - 1 + 2 * (n_gy - 1))
-
-            @pl.when(jnp.logical_not(edge))
+                pl.semaphore_wait(barrier, plane + nz - 1 + n_gy - 1)
+
+            @pl.when(jnp.logical_and(outer, jnp.logical_not(edge)))
             def _():
-                pl.semaphore_wait(barrier, n_gx - 1 + n_gy - 1)
-
-        @pl.when(edge)
-        def _():
-            mine = jnp.where(edge_e, bnd[0:rows], bnd[rows : 2 * rows])
-            if step == 0:
+                pl.semaphore_wait(barrier, plane + nz - 1)
+
+            @pl.when(jnp.logical_not(outer))
+            def _():
+                pl.semaphore_wait(barrier, plane + nz - 2)
+
+        if step == 0:
+            @pl.when(edge)
+            def _():
                 loads[2].wait()
                 loads[3].wait()
-                for q, value in enumerate((mine, h_v[column(x0), :], d_v[column(x0), :], h_v[column(x1), :])):
+                for q, (ref, x) in enumerate(
+                    ((r_v, x0), (r_v, x1), (r_v, x2), (h_v, x0), (h_v, x1), (d_v, x0), (d_v, x1))
+                ):
+                    strip[q, 8 : 8 + rows, :] = ref[column(x), :]
+
+                @pl.when(gy < n_gy - 1)
+                def _():
+                    strip_up.start()
+
+                @pl.when(gy > 0)
+                def _():
+                    strip_down.start()
+
+                mine = jnp.where(edge_e, bnd[0:rows], bnd[rows : 2 * rows])
+                for q, value in enumerate((mine, strip[3, 8 : 8 + rows, :])):
                     pack_a[q] = value
                     own_a[q, chip, core] = value
-                spread(0, pack_a, pack_a.at[pl.ds(0, 3)], own_a, opp_a)
-            elif step == 1:
-                pack_z[0] = mine
-                own_b[0, chip, core] = mine
-                spread(1, pack_z.at[pl.ds(0, 1)], pack_z.at[pl.ds(0, 1)], own_b, opp_b)
-            else:
-                pack_z[1] = mine
+                spread(0, pack_a, pack_a, own_a, opp_a)
+                pack_d[...] = strip[5, 8 : 8 + rows, :]
+                own_d[chip, core] = strip[5, 8 : 8 + rows, :]
                 for k in far_first:
                     for c in range(2):
-                        to = 2 * lax.rem(chip + k, chips) + c
-                        remote(pack_z.at[1], opp_c.at[chip, core], ss_x.at[2, 0], rs_x.at[2, 0], (across, to)).start()
+                        if k or c:
+                            to = 2 * lax.rem(chip + k, chips) + lax.rem(core + c, 2)
+                            remote(pack_d, own_d.at[chip, core], ss_d, rs_d, (gx, to)).start()
 
         to_east = remote(send_e.at[step], hal_w.at[step], ss_e.at[step], rs_w.at[step], (east, gy))
         to_west = remote(send_w.at[step], hal_e.at[step], ss_w.at[step], rs_e.at[step], (west, gy))
@@ -257,7 +348,20 @@
                 weights(m2_v, w2_hi, w2_lo)
                 row = er_v[pl.ds(table, 1), :]
                 hit = lax.broadcasted_iota(jnp.int32, (full, full), 0) == row
-                perm[...] = jnp.where(hit, 1.0, 0.0).T.astype(BF16)
+                one = jnp.where(hit, 1.0, 0.0).T
+                perm[...] = one.astype(BF16)
+                perm_w[8 : 8 + full, :] = one
+
+                @pl.when(gy < n_gy - 1)
+                def _():
+                    strip_down.wait_recv()
+
+                @pl.when(gy > 0)
+                def _():
+                    strip_up.wait_recv()
+
+                run_strip()
+                spread(1, pack_b.at[pl.ds(0, 1)], pack_b, own_b, opp_b)
 
         row = lax.broadcasted_iota(jnp.int32, (cols, lev), 0)
         for y in range(rows):
@@ -276,6 +380,9 @@
         if step == ITERS - 1:
             @pl.when(edge)
             def _():
+                arrived(d2s_v.at[pl.ds(0, (n_gy - 1) * rows)], rs_d)
+                pack_g[...] = met(perm[block, :], own_d[...].reshape(full, lev))
+                remote(pack_g, opp_g, ss_g, rs_g, (across, gy)).start()
                 hand_over(0, own_a, opp_a)
 
         @pl.when(gy < n_gy - 1)
@@ -305,13 +412,7 @@
     @pl.when(edge)
     def _():
         def whole(ref, *at):
-            return ref[at].reshape(full, lev) if at else ref[...].reshape(full, lev)
-
-        def met(x, which=None):
-            a, b = split(x)
-            matrix = perm[...] if which is None else perm[which, :]
-            out = jnp.dot(matrix, jnp.concatenate([a, b], 1), preferred_element_type=F32)
-            return out[:, :lev] + out[:, lev:]
+            return ref[at].reshape(full, lev)
 
         line = lax.broadcasted_iota(jnp.int32, (full, lev), 0)
 
@@ -319,57 +420,50 @@
             up = jnp.where(line == full - 1, 0.0, pltpu.roll(x, full - 1, 0))
             return up + jnp.where(line == 0, 0.0, pltpu.roll(x, 1, 0))
 
-        def on_line(d, h, both):
-            x = both[:, :lev]
-            return (d + 4.0 * h) * x + both[:, lev:] - h * along(x)
-
+        hand_over(1, own_b, opp_b)
         handed(0, own_a, opp_a)
-        hs, ds, h1 = whole(own_a, 1), whole(own_a, 2), whole(own_a, 3)
-        ho, do = whole(opp_a, 1), whole(opp_a, 2)
-        c1s = -hs * met(whole(opp_a, 0))
+        hs, ho = whole(own_a, 1), whole(opp_a, 1)
+        c1s = -hs * met(perm[...], whole(opp_a, 0))
         c1s_v[...] = c1s
         two = times(c1s, 2 * lev)
-        d2s = two[:, :lev]
-        d2s_v[...] = d2s
-        l2s_v[...] = on_line(ds, hs, two)
-        k1 = -h1 * d2s
-        k1_v[...] = k1
+        d2s_v[8 : 8 + full, :] = two[:, :lev]
+        t2s_v[8 : 8 + full, :] = two[:, lev:]
+        c1o = -ho * met(perm[...], whole(own_a, 0))
+        two = times(c1o, 2 * lev, True)
+        d2o = two[:, :lev]
+        d2o_v[...] = d2o
+        l2o_v[...] = 4.0 * ho * d2o + two[:, lev:] - ho * along(d2o)
+        ha, hb, da, db = strip[3], strip[4], strip[5], strip[6]
+        d2s = d2s_v[near, :]
+        l2s = window_line(da, ha, d2s, t2s_v[near, :])
+        k1 = -hb * d2s
         two = times(k1, 2 * lev)
-        d31_v[...] = two[:, :lev]
-        l31_v[...] = two[:, lev:]
-        c1o = -ho * met(whole(own_a, 0))
-        two = times(c1o, 2 * lev, True)
-        d2o_v[...] = two[:, :lev]
-        l2o_v[...] = on_line(do, ho, two)
-
-        hand_over(1, own_b, opp_b)
+        d31 = two[:, :lev]
+        l31 = window_line(db, hb, d31, two[:, lev:])
+
         handed(1, own_b, opp_b)
-        hs, ho = whole(own_a, 1), whole(opp_a, 1)
-        k2s = l2s_v[...] - hs * met(whole(opp_b, 0) + d2o_v[...])
-        k2s_v[...] = k2s
-        k2o = l2o_v[...] - ho * met(whole(own_b, 0) + d2s_v[...])
-        d3o_v[...] = times(k2o, lev, True)
+        k2s = l2s - ha * met(perm_w[near, :].astype(BF16), whole(opp_b, 0) + d2o_v[...])
         two = times(k2s, 2 * lev)
-        d3s_v[...] = two[:, :lev]
-        l3s_v[...] = on_line(whole(own_a, 2), hs, two)
-        l31_v[...] = l31_v[...] - whole(own_a, 3) * (along(d31_v[...]) + d3s_v[...])
-
-        here = pl.ds(pl.multiple_of(gy * rows, rows), rows)
+        d3s = two[:, :lev]
+        l3s = window_line(da, ha, d3s, two[:, lev:])
+        k2o = l2o_v[...] - whole(opp_a, 1) * met(perm[...], whole(own_b, 0) + d2s_v[8 : 8 + full, :])
+        k2o, d2o, z3o = met(perm[block, :], k2o, d2o_v[...], whole(opp_b, 1))
+        arrived(opp_g, rs_g)
+        z3o = z3o + times(k2o + opp_g[...] * d2o, lev, True)
+
         c0, c1, c2 = column(x0), column(x1), column(x2)
         p0, p1 = column(x0, pad), column(x1, pad)
-        d3s, d31 = d3s_v[here, :], d31_v[here, :]
-        h0, h_1 = h_v[c0, :], h_v[c1, :]
-        u_v[0, c0, :] = u_v[0, c0, :] + c1s_v[here, :]
-        u_v[1, c0, :] = u_v[1, c0, :] + k2s_v[here, :]
-        u_v[1, c1, :] = u_v[1, c1, :] + k1_v[here, :]
-        z_v[1, p0, :] = z_v[1, p0, :] + d2s_v[here, :]
-        z_v[2, p0, :] = z_v[2, p0, :] + d3s
-        z_v[2, p1, :] = z_v[2, p1, :] + d31
-        u_v[2, c1, :] = u_v[2, c1, :] + (d_v[c1, :] + 4.0 * h_1) * d31 + l31_v[here, :]
-        u_v[2, c2, :] = u_v[2, c2, :] - h_v[c2, :] * d31
-        partial = u_v[2, c0, :] + l3s_v[here, :] - h0 * d31
-        arrived(opp_c, rs_x.at[2, 0])
-        u_v[2, c0, :] = partial - h0 * met(whole(opp_c) + d3o_v[...], here)
+        h0, h1 = ha[inner_rows], hb[inner_rows]
+        d31_in, d3s_in = d31[inner_rows], d3s[inner_rows]
+        u_v[0, c0, :] = u_v[0, c0, :] + c1s_v[block, :]
+        u_v[1, c0, :] = u_v[1, c0, :] + k2s[inner_rows]
+        u_v[1, c1, :] = u_v[1, c1, :] + k1[inner_rows]
+        z_v[1, p0, :] = z_v[1, p0, :] + d2s[inner_rows]
+        z_v[2, p0, :] = z_v[2, p0, :] + d3s_in
+        z_v[2, p1, :] = z_v[2, p1, :] + d31_in
+        u_v[2, c0, :] = u_v[2, c0, :] + l3s[inner_rows] - h0 * (d31_in + z3o)
+        u_v[2, c1, :] = u_v[2, c1, :] + l31[inner_rows] - h1 * d3s_in
+        u_v[2, c2, :] = u_v[2, c2, :] - h_v[c2, :] * d31_in
 
     for i in range(ITERS + 1):
         for j in range(i, ITERS + 1):
@@ -398,8 +492,8 @@
         pltpu.make_async_copy(recv, recv, rs).wait()
         return part[...] + jnp.sum(recv[...], 0, keepdims=True)
 
-    part2[...] = share(part1, recv1, ss_1, rs_1, n_gy, gy, lambda p: (gx, p))
-    total = share(part2, recv2, ss_2, rs_2, n_gx, gx, lambda p: (p, gy))
+    part2[...] = share(part1, recv1, ss_1, rs_1, plane, in_plane, at_plane)
+    total = share(part2, recv2, ss_2, rs_2, nz, z_, at_line)
     total = total.reshape(1, lev) * (1.0 / total_cells)
     lane1 = lax.broadcasted_iota(jnp.int32, (1, lev), 1)
     g = {}
@@ -446,8 +540,17 @@
     @pl.when(edge)
     def _():
         sent(0, pack_a, pack_a, own_a, opp_a)
-        sent(1, pack_z, pack_z, own_b, opp_b)
-        arrived(opp_c, ss_x.at[2, 0])
+        sent(1, pack_b, pack_b, own_b, opp_b)
+        arrived(d2s_v.at[pl.ds(0, (n_gy - 1) * rows)], ss_d)
+        arrived(pack_g, ss_g)
+
+        @pl.when(gy < n_gy - 1)
+        def _():
+            strip_up.wait_send()
+
+        @pl.when(gy > 0)
+        def _():
+            strip_down.wait_send()
 
     pltpu.make_async_copy(recv1, recv1, ss_1).wait()
     pltpu.make_async_copy(recv2, recv2, ss_2).wait()
@@ -477,6 +580,7 @@
     dma = pltpu.SemaphoreType.DMA
     full = n_gy * rows
     chips = n_gy // 2
+    ny = 4 if n_gx % 4 == 0 else 2
     scratch = [
         *[pltpu.VMEM((cells, lev), F32)] * 3,
         pltpu.VMEM((1, lev), F32),
@@ -490,27 +594,32 @@
         *[pltpu.VMEM((ITERS, cols, lev), F32)] * 2,
         *[pltpu.VMEM((ITERS, rows, lev), F32)] * 2,
         *[pltpu.VMEM((ITERS, cols, lev), F32)] * 2,
-        pltpu.VMEM((4, rows, lev), F32),
-        pltpu.VMEM((2, rows, lev), F32),
-        pltpu.VMEM((4, chips, 2, rows, lev), F32),
-        pltpu.VMEM((3, chips, 2, rows, lev), F32),
+        *[pltpu.VMEM((2, rows, lev), F32)] * 2,
+        *[pltpu.VMEM((rows, lev), F32)] * 2,
+        *[pltpu.VMEM((2, chips, 2, rows, lev), F32)] * 2,
         pltpu.VMEM((1, chips, 2, rows, lev), F32),
-        pltpu.VMEM((1, chips, 2, rows, lev), F32),
+        pltpu.VMEM((2, chips, 2, rows, lev), F32),
         pltpu.VMEM((chips, 2, rows, lev), F32),
+        pltpu.VMEM((rows, lev), F32),
+        pltpu.VMEM((7, rows + 16, lev), F32),
         pltpu.VMEM((full, full), BF16),
-        *[pltpu.VMEM((full, lev), F32)] * 12,
+        pltpu.VMEM((full + 16, full), F32),
+        pltpu.VMEM((full, lev), F32),
+        *[pltpu.VMEM((full + 16, lev), F32)] * 2,
+        *[pltpu.VMEM((full, lev), F32)] * 2,
         pltpu.VMEM((1, 1, lev), F32),
         pltpu.VMEM((1, 1, lev), F32),
-        pltpu.VMEM((n_gy - 1, 1, lev), F32),
-        pltpu.VMEM((n_gx - 1, 1, lev), F32),
+        pltpu.VMEM((ny * n_gy - 1, 1, lev), F32),
+        pltpu.VMEM((n_gx // ny - 1, 1, lev), F32),
         dma((7,)),
         dma((ITERS,)), dma((ITERS,)), dma((ITERS,)), dma((ITERS,)),
         dma((ITERS,)), dma((ITERS,)), dma((ITERS,)), dma((ITERS,)),
-        dma((3, 2)), dma((3, 2)), dma((2, 2)), dma((2, 2)),
+        dma((2, 2)), dma((2, 2)), dma((2, 2)), dma((2, 2)),
+        dma((2,)), dma((2,)), dma, dma, dma, dma,
         dma, dma, dma, dma,
     ]
     x, res, sq = pl.pallas_call(
-        functools.partial(kernel, n_gx, n_gy, rows, cols),
+        functools.partial(kernel, n_gx, n_gy, ny, rows, cols),
         out_shape=(
             pltpu.VMEM((cells, lev), F32),
             pltpu.VMEM((cells, lev), F32),

time: 35.5 us -> 33.8 us (0.952)
  Pallas kernels: 34.7 us -> 33.1 us
    pallas_call x1, Pallas kernels: 33.9 us -> 32.3 us  [on_device(): pl.pallas_call(functools.partial(kernel, n_gx, n_gy, ny, rows, cols), out...]
where the time goes in v4:
time: 33.8 us; the launch traced here: 33.7 us
  Pallas kernels  33.1 us (98%)
  between operations  0.64 us (2%)
    pallas_call x1, Pallas kernels, on_device(): pl.pallas_call(functools.partial(kernel, n_gx, n_gy, ny, rows, cols), out...  32.3 us
    pallas_call x1, Pallas kernels, on_device(): pl.pallas_call(write_out, out_shape=(jax.ShapeDtypeStruct((cells, lev), F...  0.83 us

profile of v4, /device:TPU:1, one launch (start us, length us, event | category | flops | bytes accessed | tf_op | source)
XLA Modules:
  0.0 33.7 jit_solution(6273163163014452803)
XLA Ops:
  0.6 32.3 %solve.1 = (f32[512,128]{1,0:T(8,128)S(1)}, f32[512,128]{1,0:T(8,128)S(1)}, f32[1,128]{1,0:T(1,128)S(1)}) custom-call(f32[512,128]{1,0:T(8,128)} %bitcast.6, f32[512,128]{1,0:T(8,128)} %bitcast.7, f32[512,128]{1,0:T(8,128)} %bitcast.8, f32[1,128]{1,0:T(1,128)} %bitcast.9, f32[2,128,128]{2,1,0:T(8,128)} %m_hbm.1, s32[2,256]{1,0:T(2,128)} %er_hbm.1), custom_call_target="tpu_custom_call" | custom-call | tf_op jit(solution)/shard_map/solve/pallas_call | solution.py:621
  32.9 0.8 %put.1 = (f32[512,128]{1,0:T(8,128)}, f32[512,128]{1,0:T(8,128)}, f32[3]{0:T(128)}) custom-call(f32[512,128]{1,0:T(8,128)S(1)} %get-tuple-element.9.x_v, f32[512,128]{1,0:T(8,128)S(1)} %get-tuple-element.10.o_v, f32[1,128]{1,0:T(1,128)S(1)} %get-tuple-element.11.sq_v), custom_call_target="tpu_custom_call" | custom-call | tf_op jit(solution)/shard_map/put/pallas_call | solution.py:634

commit v5 on v4

--- a/solution.py
+++ b/solution.py
@@ -25,7 +25,7 @@
     r_v, d_v, h_v, vert_ref, m_v, m2_v, er_v, w_hi, w_lo, w2_hi, w2_lo, z_v, u_v, t_v,
     send_e, send_w, send_n, send_s, hal_e, hal_w, hal_n, hal_s,
     pack_a, pack_b, pack_d, pack_g, own_a, opp_a, own_b, opp_b, own_d, opp_g, strip, perm, perm_w,
-    c1s_v, d2s_v, t2s_v, d2o_v, l2o_v,
+    c1s_v, d2s_v, t2s_v, d2o_v, perm2, gram_v,
     part1, part2, recv1, recv2,
     ld_sem, ss_e, ss_w, ss_n, ss_s, rs_e, rs_w, rs_n, rs_s, ss_x, rs_x, fs_x, fr_x, ss_t, rs_t, ss_d, rs_d, ss_g, rs_g, ss_1, ss_2, rs_1, rs_2,
 ):
@@ -175,18 +175,22 @@
     def spread(number, pack_own, pack_opp, own, opp):
         for k in far_first:
             to = 2 * lax.rem(chip + k, chips) + core
-            remote(pack_opp, opp.at[:, chip, core], ss_x.at[number, 0], rs_x.at[number, 0], (across, to)).start()
+            remote(pack_opp, opp.at[:, chip, core], ss_x.at[number, 0], rs_x.at[number, 0, k], (across, to)).start()
             if k:
-                remote(pack_own, own.at[:, chip, core], ss_x.at[number, 1], rs_x.at[number, 1], (gx, to)).start()
+                remote(pack_own, own.at[:, chip, core], ss_x.at[number, 1], rs_x.at[number, 1, k], (gx, to)).start()
 
     def arrived(ref, sem):
         pltpu.make_async_copy(ref, ref, sem).wait()
 
     def hand_over(number, own, opp):
         sibling = (gx, gy + 1 - 2 * core)
-        for which, buf in ((0, opp), (1, own)):
-            arrived(buf.at[:, pl.ds(0, chips - which), core], rs_x.at[number, which])
-            remote(buf.at[:, :, core], buf.at[:, :, core], fs_x.at[number, which], fr_x.at[number, which], sibling).start()
+        for k in reversed(far_first):
+            origin = lax.rem(chip + chips - k, chips)
+            for which, buf in ((0, opp), (1, own)):
+                part = buf.at[:, origin, core]
+                if k or not which:
+                    arrived(part, rs_x.at[number, which, k])
+                remote(part, part, fs_x.at[number, which], fr_x.at[number, which], sibling).start()
 
     def handed(number, own, opp):
         for which, buf in ((0, opp), (1, own)):
@@ -198,13 +202,16 @@
         arrived(opp.at[:, :, core], fs_x.at[number, 0])
         arrived(own.at[:, :, core], fs_x.at[number, 1])
 
-    grams = {}
-
-    def field(i):
-        return r_v[...] if i == 0 else u_v[i - 1]
-
-    def accumulate(i, j):
-        grams[(i, j)] = jnp.sum((field(i) * field(j)).reshape(cells // 8, 8, lev), 0)
+    keys = [(i, j) for j in range(ITERS + 1) for i in range(j + 1)]
+    spot = lax.broadcasted_iota(jnp.int32, (cols, lev), 0)
+    strip_cols = (spot == x0) | (spot == x1) | (spot == x2)
+    weight = jnp.where(jnp.logical_and(strip_cols, edge), 0.0, 1.0)
+
+    def accumulate(j):
+        field = [r_v[...] if i == 0 else u_v[i - 1] for i in range(j + 1)]
+        masked = (field[j].reshape(rows, cols, lev) * weight[None]).reshape(cells, lev)
+        for i in range(j + 1):
+            gram_v[keys.index((i, j))] = jnp.sum((field[i] * masked).reshape(cells // 8, 8, lev), 0)
 
     strip_up = remote(
         strip.at[:, pl.ds(rows, 8)], strip.at[:, pl.ds(0, 8)], ss_t.at[0], rs_t.at[0], (gx, lax.rem(gy + 1, n_gy))
@@ -270,6 +277,36 @@
             def _():
                 pl.semaphore_wait(barrier, plane + nz - 2)
 
+        to_east = remote(send_e.at[step], hal_w.at[step], ss_e.at[step], rs_w.at[step], (east, gy))
+        to_west = remote(send_w.at[step], hal_e.at[step], ss_w.at[step], rs_e.at[step], (west, gy))
+
+        @pl.when(jnp.logical_not(edge_e))
+        def _():
+            to_east.start()
+
+        @pl.when(jnp.logical_not(edge_w))
+        def _():
+            to_west.start()
+
+        north = pltpu.make_async_remote_copy(
+            src_ref=send_n.at[step], dst_ref=hal_s.at[step],
+            send_sem=ss_n.at[step], recv_sem=rs_s.at[step],
+            device_id=(gx, lax.rem(gy + 1, n_gy)), device_id_type=MESH,
+        )
+        south = pltpu.make_async_remote_copy(
+            src_ref=send_s.at[step], dst_ref=hal_n.at[step],
+            send_sem=ss_s.at[step], recv_sem=rs_n.at[step],
+            device_id=(gx, lax.rem(gy + n_gy - 1, n_gy)), device_id_type=MESH,
+        )
+
+        @pl.when(gy < n_gy - 1)
+        def _():
+            north.start()
+
+        @pl.when(gy > 0)
+        def _():
+            south.start()
+
         if step == 0:
             @pl.when(edge)
             def _():
@@ -301,36 +338,6 @@
                             to = 2 * lax.rem(chip + k, chips) + lax.rem(core + c, 2)
                             remote(pack_d, own_d.at[chip, core], ss_d, rs_d, (gx, to)).start()
 
-        to_east = remote(send_e.at[step], hal_w.at[step], ss_e.at[step], rs_w.at[step], (east, gy))
-        to_west = remote(send_w.at[step], hal_e.at[step], ss_w.at[step], rs_e.at[step], (west, gy))
-
-        @pl.when(jnp.logical_not(edge_e))
-        def _():
-            to_east.start()
-
-        @pl.when(jnp.logical_not(edge_w))
-        def _():
-            to_west.start()
-
-        north = pltpu.make_async_remote_copy(
-            src_ref=send_n.at[step], dst_ref=hal_s.at[step],
-            send_sem=ss_n.at[step], recv_sem=rs_s.at[step],
-            device_id=(gx, lax.rem(gy + 1, n_gy)), device_id_type=MESH,
-        )
-        south = pltpu.make_async_remote_copy(
-            src_ref=send_s.at[step], dst_ref=hal_n.at[step],
-            send_sem=ss_s.at[step], recv_sem=rs_n.at[step],
-            device_id=(gx, lax.rem(gy + n_gy - 1, n_gy)), device_id_type=MESH,
-        )
-
-        @pl.when(gy < n_gy - 1)
-        def _():
-            north.start()
-
-        @pl.when(gy > 0)
-        def _():
-            south.start()
-
         both = times(src[...], 2 * lev)
         z_v[step, pad : pad + cells, :] = both[:, :lev]
         t_v[...] = both[:, lev:]
@@ -351,6 +358,7 @@
                 one = jnp.where(hit, 1.0, 0.0).T
                 perm[...] = one.astype(BF16)
                 perm_w[8 : 8 + full, :] = one
+                perm2[...] = jnp.dot(perm[block, :], perm[...], preferred_element_type=F32).astype(BF16)
 
                 @pl.when(gy < n_gy - 1)
                 def _():
@@ -385,6 +393,8 @@
                 remote(pack_g, opp_g, ss_g, rs_g, (across, gy)).start()
                 hand_over(0, own_a, opp_a)
 
+        accumulate(step)
+
         @pl.when(gy < n_gy - 1)
         def _():
             south.wait_recv()
@@ -408,6 +418,8 @@
 
         u_v[step, last, :] = u_v[step, last, :] - h_v[last, :] * hal_e[step]
         u_v[step, first, :] = u_v[step, first, :] - h_v[first, :] * hal_w[step]
+
+    accumulate(ITERS)
 
     @pl.when(edge)
     def _():
@@ -432,7 +444,8 @@
         two = times(c1o, 2 * lev, True)
         d2o = two[:, :lev]
         d2o_v[...] = d2o
-        l2o_v[...] = 4.0 * ho * d2o + two[:, lev:] - ho * along(d2o)
+        l2o = 4.0 * ho * d2o + two[:, lev:] - ho * along(d2o)
+        ho, d2o, l2o = met(perm[block, :], ho, d2o, l2o)
         ha, hb, da, db = strip[3], strip[4], strip[5], strip[6]
         d2s = d2s_v[near, :]
         l2s = window_line(da, ha, d2s, t2s_v[near, :])
@@ -446,10 +459,10 @@
         two = times(k2s, 2 * lev)
         d3s = two[:, :lev]
         l3s = window_line(da, ha, d3s, two[:, lev:])
-        k2o = l2o_v[...] - whole(opp_a, 1) * met(perm[...], whole(own_b, 0) + d2s_v[8 : 8 + full, :])
-        k2o, d2o, z3o = met(perm[block, :], k2o, d2o_v[...], whole(opp_b, 1))
+        z2s = met(perm2[...], whole(own_b, 0) + d2s_v[8 : 8 + full, :])
+        z3o = met(perm[block, :], whole(opp_b, 1))
         arrived(opp_g, rs_g)
-        z3o = z3o + times(k2o + opp_g[...] * d2o, lev, True)
+        z3o = z3o + times(l2o + opp_g[...] * d2o - ho * z2s, lev, True)
 
         c0, c1, c2 = column(x0), column(x1), column(x2)
         p0, p1 = column(x0, pad), column(x1, pad)
@@ -464,13 +477,15 @@
         u_v[2, c0, :] = u_v[2, c0, :] + l3s[inner_rows] - h0 * (d31_in + z3o)
         u_v[2, c1, :] = u_v[2, c1, :] + l31[inner_rows] - h1 * d3s_in
         u_v[2, c2, :] = u_v[2, c2, :] - h_v[c2, :] * d31_in
-
-    for i in range(ITERS + 1):
-        for j in range(i, ITERS + 1):
-            accumulate(i, j)
-
-    keys = [(i, j) for j in range(ITERS + 1) for i in range(j + 1)]
-    stack = jnp.concatenate([jnp.sum(grams[key], 0, keepdims=True) for key in keys], 0)
+        thin = [
+            jnp.concatenate([ref[c, :] for c in (c0, c1, c2)], 0)
+            for ref in (r_v, u_v.at[0], u_v.at[1], u_v.at[2])
+        ]
+        for n, (i, j) in enumerate(keys):
+            gram_v[n] = gram_v[n] + jnp.sum((thin[i] * thin[j]).reshape(3 * rows // 8, 8, lev), 0)
+
+
+    stack = jnp.sum(gram_v[...], 1)
     sums = jnp.sum(stack, 1, keepdims=True)
     n = len(keys)
     pick = lax.broadcasted_iota(jnp.int32, (n, lev), 0) == lax.broadcasted_iota(jnp.int32, (n, lev), 1)
@@ -606,7 +621,9 @@
         pltpu.VMEM((full + 16, full), F32),
         pltpu.VMEM((full, lev), F32),
         *[pltpu.VMEM((full + 16, lev), F32)] * 2,
-        *[pltpu.VMEM((full, lev), F32)] * 2,
+        pltpu.VMEM((full, lev), F32),
+        pltpu.VMEM((rows, full), BF16),
+        pltpu.VMEM(((ITERS + 1) * (ITERS + 2) // 2, 8, lev), F32),
         pltpu.VMEM((1, 1, lev), F32),
         pltpu.VMEM((1, 1, lev), F32),
         pltpu.VMEM((ny * n_gy - 1, 1, lev), F32),
@@ -614,7 +631,7 @@
         dma((7,)),
         dma((ITERS,)), dma((ITERS,)), dma((ITERS,)), dma((ITERS,)),
         dma((ITERS,)), dma((ITERS,)), dma((ITERS,)), dma((ITERS,)),
-        dma((2, 2)), dma((2, 2)), dma((2, 2)), dma((2, 2)),
+        dma((2, 2)), dma((2, 2, n_gy // 2)), dma((2, 2)), dma((2, 2)),
         dma((2,)), dma((2,)), dma, dma, dma, dma,
         dma, dma, dma, dma,
     ]

time: 33.8 us -> 33.1 us (0.979)
  Pallas kernels: 33.1 us -> 32.3 us
    pallas_call x1, Pallas kernels: 32.3 us -> 31.5 us  [on_device(): pl.pallas_call(functools.partial(kernel, n_gx, n_gy, ny, rows, cols), out...]
where the time goes in v5:
time: 33.1 us; the launch traced here: 33 us
  Pallas kernels  32.3 us (98%)
  between operations  0.64 us (2%)
    pallas_call x1, Pallas kernels, on_device(): pl.pallas_call(functools.partial(kernel, n_gx, n_gy, ny, rows, cols), out...  31.5 us
    pallas_call x1, Pallas kernels, on_device(): pl.pallas_call(write_out, out_shape=(jax.ShapeDtypeStruct((cells, lev), F...  0.83 us

profile of v5, /device:TPU:1, one launch (start us, length us, event | category | flops | bytes accessed | tf_op | source)
XLA Modules:
  0.0 33.0 jit_solution(11170136670458456480)
XLA Ops:
  0.6 31.5 %solve.1 = (f32[512,128]{1,0:T(8,128)S(1)}, f32[512,128]{1,0:T(8,128)S(1)}, f32[1,128]{1,0:T(1,128)S(1)}) custom-call(f32[512,128]{1,0:T(8,128)} %bitcast.6, f32[512,128]{1,0:T(8,128)} %bitcast.7, f32[512,128]{1,0:T(8,128)} %bitcast.8, f32[1,128]{1,0:T(1,128)} %bitcast.9, f32[2,128,128]{2,1,0:T(8,128)} %m_hbm.1, s32[2,256]{1,0:T(2,128)} %er_hbm.1), custom_call_target="tpu_custom_call" | custom-call | tf_op jit(solution)/shard_map/solve/pallas_call | solution.py:638
  32.1 0.8 %put.1 = (f32[512,128]{1,0:T(8,128)}, f32[512,128]{1,0:T(8,128)}, f32[3]{0:T(128)}) custom-call(f32[512,128]{1,0:T(8,128)S(1)} %get-tuple-element.9.x_v, f32[512,128]{1,0:T(8,128)S(1)} %get-tuple-element.10.o_v, f32[1,128]{1,0:T(1,128)S(1)} %get-tuple-element.11.sq_v), custom_call_target="tpu_custom_call" | custom-call | tf_op jit(solution)/shard_map/put/pallas_call | solution.py:651

commit v6 on v5

--- a/solution.py
+++ b/solution.py
@@ -1,4 +1,5 @@
 import functools
+import itertools
 
 import jax
 import jax.numpy as jnp
@@ -27,7 +28,7 @@
     pack_a, pack_b, pack_d, pack_g, own_a, opp_a, own_b, opp_b, own_d, opp_g, strip, perm, perm_w,
     c1s_v, d2s_v, t2s_v, d2o_v, perm2, gram_v,
     part1, part2, recv1, recv2,
-    ld_sem, ss_e, ss_w, ss_n, ss_s, rs_e, rs_w, rs_n, rs_s, ss_x, rs_x, fs_x, fr_x, ss_t, rs_t, ss_d, rs_d, ss_g, rs_g, ss_1, ss_2, rs_1, rs_2,
+    ld_sem, ss_e, ss_w, ss_n, ss_s, rs_e, rs_w, rs_n, rs_s, ss_x, rs_x, fs_x, fr_x, ss_t, rs_t, ss_d, rs_d, ss_g, rs_g, ss_1, ss_2, rs_1, rs_2, ready,
 ):
     gx = lax.axis_index("gx")
     gy = lax.axis_index("gy")
@@ -79,6 +80,18 @@
     def at_line(p):
         return (p * ny + y_, gy)
 
+    def far(offset):
+        return -sum(min(o, n - o) for o, n in zip(offset, (nz, ny, chips)))
+
+    def peer(offset):
+        oz, oy, ox, oc = offset
+        at = lax.rem(z_ + oz, nz) * ny + lax.rem(y_ + oy, ny)
+        return (at, 2 * lax.rem(chip + ox, chips) + lax.rem(core + oc, 2))
+
+    every = sorted(itertools.product(range(nz), range(ny), range(chips), range(2)), key=far)
+    every.remove((0, 0, 0, 0))
+    others = [offset for offset in every if not offset[3]]
+
     barrier = pltpu.get_barrier_semaphore()
 
     def greet(device):
@@ -287,6 +300,10 @@
         @pl.when(jnp.logical_not(edge_w))
         def _():
             to_west.start()
+
+        if step == 0:
+            for i in range(1, nz):
+                pl.semaphore_signal(ready, inc=1, device_id=at_line(lax.rem(z_ + i, nz)), device_id_type=MESH)
 
         north = pltpu.make_async_remote_copy(
             src_ref=send_n.at[step], dst_ref=hal_s.at[step],
@@ -491,24 +508,15 @@
     pick = lax.broadcasted_iota(jnp.int32, (n, lev), 0) == lax.broadcasted_iota(jnp.int32, (n, lev), 1)
     part1[...] = jnp.sum(jnp.where(pick, sums, 0.0), 0, keepdims=True).reshape(1, 1, lev)
 
-    def share(part, recv, ss, rs, count, me, device):
-        copies = []
-        for i in range(1, count):
-            peer = lax.rem(me + i, count)
-            copies.append(
-                pltpu.make_async_remote_copy(
-                    src_ref=part, dst_ref=recv.at[pl.ds(count - 1 - i, 1)],
-                    send_sem=ss, recv_sem=rs,
-                    device_id=device(peer), device_id_type=MESH,
-                )
-            )
-        for c in copies:
-            c.start()
+    def share(part, recv, ss, rs, offsets):
+        for n, offset in enumerate(offsets):
+            remote(part, recv.at[pl.ds(n, 1)], ss, rs, peer(offset)).start()
         pltpu.make_async_copy(recv, recv, rs).wait()
         return part[...] + jnp.sum(recv[...], 0, keepdims=True)
 
-    part2[...] = share(part1, recv1, ss_1, rs_1, plane, in_plane, at_plane)
-    total = share(part2, recv2, ss_2, rs_2, nz, z_, at_line)
+    pl.semaphore_wait(ready, nz - 1)
+    part2[...] = share(part1, recv1, ss_1, rs_1, [(0, 0, 0, 1)])
+    total = share(part2, recv2, ss_2, rs_2, others)
     total = total.reshape(1, lev) * (1.0 / total_cells)
     lane1 = lax.broadcasted_iota(jnp.int32, (1, lev), 1)
     g = {}
@@ -626,14 +634,14 @@
         pltpu.VMEM(((ITERS + 1) * (ITERS + 2) // 2, 8, lev), F32),
         pltpu.VMEM((1, 1, lev), F32),
         pltpu.VMEM((1, 1, lev), F32),
-        pltpu.VMEM((ny * n_gy - 1, 1, lev), F32),
-        pltpu.VMEM((n_gx // ny - 1, 1, lev), F32),
+        pltpu.VMEM((1, 1, lev), F32),
+        pltpu.VMEM((n_gx * n_gy // 2 - 1, 1, lev), F32),
         dma((7,)),
         dma((ITERS,)), dma((ITERS,)), dma((ITERS,)), dma((ITERS,)),
         dma((ITERS,)), dma((ITERS,)), dma((ITERS,)), dma((ITERS,)),
         dma((2, 2)), dma((2, 2, n_gy // 2)), dma((2, 2)), dma((2, 2)),
         dma((2,)), dma((2,)), dma, dma, dma, dma,
-        dma, dma, dma, dma,
+        dma, dma, dma, dma, pltpu.SemaphoreType.REGULAR,
     ]
     x, res, sq = pl.pallas_call(
         functools.partial(kernel, n_gx, n_gy, ny, rows, cols),

time: 33.1 us -> 32.5 us (0.982)
  Pallas kernels: 32.3 us -> 31.8 us
    pallas_call x1, Pallas kernels: 31.5 us -> 31 us  [on_device(): pl.pallas_call(functools.partial(kernel, n_gx, n_gy, ny, rows, cols), out...]
where the time goes in v6:
time: 32.5 us; the launch traced here: 32.4 us
  Pallas kernels  31.8 us (98%)
  between operations  0.64 us (2%)
    pallas_call x1, Pallas kernels, on_device(): pl.pallas_call(functools.partial(kernel, n_gx, n_gy, ny, rows, cols), out...  31 us
    pallas_call x1, Pallas kernels, on_device(): pl.pallas_call(write_out, out_shape=(jax.ShapeDtypeStruct((cells, lev), F...  0.83 us

profile of v6, /device:TPU:1, one launch (start us, length us, event | category | flops | bytes accessed | tf_op | source)
XLA Modules:
  0.0 32.4 jit_solution(14123151681509156210)
XLA Ops:
  0.6 31.0 %solve.1 = (f32[512,128]{1,0:T(8,128)S(1)}, f32[512,128]{1,0:T(8,128)S(1)}, f32[1,128]{1,0:T(1,128)S(1)}) custom-call(f32[512,128]{1,0:T(8,128)} %bitcast.6, f32[512,128]{1,0:T(8,128)} %bitcast.7, f32[512,128]{1,0:T(8,128)} %bitcast.8, f32[1,128]{1,0:T(1,128)} %bitcast.9, f32[2,128,128]{2,1,0:T(8,128)} %m_hbm.1, s32[2,256]{1,0:T(2,128)} %er_hbm.1), custom_call_target="tpu_custom_call" | custom-call | tf_op jit(solution)/shard_map/solve/pallas_call | solution.py:646
  31.6 0.8 %put.1 = (f32[512,128]{1,0:T(8,128)}, f32[512,128]{1,0:T(8,128)}, f32[3]{0:T(128)}) custom-call(f32[512,128]{1,0:T(8,128)S(1)} %get-tuple-element.9.x_v, f32[512,128]{1,0:T(8,128)S(1)} %get-tuple-element.10.o_v, f32[1,128]{1,0:T(1,128)S(1)} %get-tuple-element.11.sq_v), custom_call_target="tpu_custom_call" | custom-call | tf_op jit(solution)/shard_map/put/pallas_call | solution.py:659

commit v7 on v6

--- a/solution.py
+++ b/solution.py
@@ -22,8 +22,8 @@
 def kernel(
     n_gx, n_gy, ny, rows, cols,
     r_hbm, d_hbm, h_hbm, vert_hbm, m_hbm, er_hbm,
-    x_v, o_v, sq_ref,
-    r_v, d_v, h_v, vert_ref, m_v, m2_v, er_v, w_hi, w_lo, w2_hi, w2_lo, z_v, u_v, t_v,
+    r_v, z_v, u_v, fin_ref,
+    d_v, h_v, vert_ref, m_v, m2_v, er_v, w_hi, w_lo, w2_hi, w2_lo, t_v,
     send_e, send_w, send_n, send_s, hal_e, hal_w, hal_n, hal_s,
     pack_a, pack_b, pack_d, pack_g, own_a, opp_a, own_b, opp_b, own_d, opp_g, strip, perm, perm_w,
     c1s_v, d2s_v, t2s_v, d2o_v, perm2, gram_v,
@@ -346,7 +346,6 @@
                 for q, value in enumerate((mine, strip[3, 8 : 8 + rows, :])):
                     pack_a[q] = value
                     own_a[q, chip, core] = value
-                spread(0, pack_a, pack_a, own_a, opp_a)
                 pack_d[...] = strip[5, 8 : 8 + rows, :]
                 own_d[chip, core] = strip[5, 8 : 8 + rows, :]
                 for k in far_first:
@@ -354,6 +353,14 @@
                         if k or c:
                             to = 2 * lax.rem(chip + k, chips) + lax.rem(core + c, 2)
                             remote(pack_d, own_d.at[chip, core], ss_d, rs_d, (gx, to)).start()
+                spread(0, pack_a, pack_a, own_a, opp_a)
+
+        if step == ITERS - 1:
+            @pl.when(edge)
+            def _():
+                arrived(d2s_v.at[pl.ds(0, (n_gy - 1) * rows)], rs_d)
+                pack_g[...] = met(perm[block, :], own_d[...].reshape(full, lev))
+                remote(pack_g, opp_g, ss_g, rs_g, (across, gy)).start()
 
         both = times(src[...], 2 * lev)
         z_v[step, pad : pad + cells, :] = both[:, :lev]
@@ -405,9 +412,6 @@
         if step == ITERS - 1:
             @pl.when(edge)
             def _():
-                arrived(d2s_v.at[pl.ds(0, (n_gy - 1) * rows)], rs_d)
-                pack_g[...] = met(perm[block, :], own_d[...].reshape(full, lev))
-                remote(pack_g, opp_g, ss_g, rs_g, (across, gy)).start()
                 hand_over(0, own_a, opp_a)
 
         accumulate(step)
@@ -511,13 +515,16 @@
     def share(part, recv, ss, rs, offsets):
         for n, offset in enumerate(offsets):
             remote(part, recv.at[pl.ds(n, 1)], ss, rs, peer(offset)).start()
-        pltpu.make_async_copy(recv, recv, rs).wait()
-        return part[...] + jnp.sum(recv[...], 0, keepdims=True)
+        arrived(recv, rs)
+        terms = [part[0]] + [recv[n] for n in range(len(offsets))]
+        while len(terms) > 1:
+            terms = [a + b for a, b in zip(terms[::2], terms[1::2])] + terms[len(terms) & ~1 :]
+        return terms[0]
 
     pl.semaphore_wait(ready, nz - 1)
-    part2[...] = share(part1, recv1, ss_1, rs_1, [(0, 0, 0, 1)])
+    part2[0] = share(part1, recv1, ss_1, rs_1, [(0, 0, 0, 1)])
     total = share(part2, recv2, ss_2, rs_2, others)
-    total = total.reshape(1, lev) * (1.0 / total_cells)
+    total = total * (1.0 / total_cells)
     lane1 = lax.broadcasted_iota(jnp.int32, (1, lev), 1)
     g = {}
     for number, key in enumerate(keys):
@@ -538,10 +545,8 @@
     q0 = g[0, 0] - a0 * a0
     q1 = q0 - a1 * a1
     q2 = q1 - a2 * a2
-    sq_ref[...] = jnp.where(lane1 == 0, q0, jnp.where(lane1 == 1, q1, q2))
-
-    x_v[...] = c1 * z_v[0, pad : pad + cells, :] + c2 * z_v[1, pad : pad + cells, :] + c3 * z_v[2, pad : pad + cells, :]
-    o_v[...] = r_v[...] - c1 * u_v[0] - c2 * u_v[1] - c3 * u_v[2]
+    for n, value in enumerate((c1, c2, c3, q0, q1, q2)):
+        fin_ref[n : n + 1, :] = jnp.broadcast_to(value, (1, lev))
 
     for step in range(ITERS):
         @pl.when(jnp.logical_not(edge_e))
@@ -579,18 +584,27 @@
     pltpu.make_async_copy(recv2, recv2, ss_2).wait()
 
 
-def write_out(x_v, o_v, sq_v, x_hbm, res_hbm, sq_hbm, sq_s, sem):
-    copies = [pltpu.make_async_copy(x_v, x_hbm, sem.at[0]), pltpu.make_async_copy(o_v, res_hbm, sem.at[1])]
-    for c in copies:
-        c.start()
-    row = sq_v[...]
-    for i in range(ITERS):
-        sq_s[i] = row[0, i]
-    last = pltpu.make_async_copy(sq_s, sq_hbm, sem.at[2])
-    last.start()
+def write_out(r_v, z_v, u_v, fin, x_hbm, res_hbm, sq_hbm, x_v, o_v, sq_s, sem):
+    cells = r_v.shape[0]
+    parts = 4
+    c1, c2, c3 = fin[0:1, :], fin[1:2, :], fin[2:3, :]
+    copies = []
+    for n in range(parts):
+        at = pl.ds(n * (cells // parts), cells // parts)
+        behind = pl.ds(8 + n * (cells // parts), cells // parts)
+        x_v[at, :] = c1 * z_v[0, behind, :] + c2 * z_v[1, behind, :] + c3 * z_v[2, behind, :]
+        copies.append(pltpu.make_async_copy(x_v.at[at], x_hbm.at[at], sem.at[2 * n]))
+        copies[-1].start()
+        o_v[at, :] = r_v[at, :] - c1 * u_v[0, at, :] - c2 * u_v[1, at, :] - c3 * u_v[2, at, :]
+        copies.append(pltpu.make_async_copy(o_v.at[at], res_hbm.at[at], sem.at[2 * n + 1]))
+        copies[-1].start()
+        if n == 0:
+            for i in range(ITERS):
+                sq_s[i] = fin[3 + i, 0]
+            copies.append(pltpu.make_async_copy(sq_s, sq_hbm, sem.at[2 * parts]))
+            copies[-1].start()
     for c in copies:
         c.wait()
-    last.wait()
 
 
 def on_device(n_gx, n_gy, right_side, diagonal, horizontal, vertical, precond, edge_rows):
@@ -605,13 +619,11 @@
     chips = n_gy // 2
     ny = 4 if n_gx % 4 == 0 else 2
     scratch = [
-        *[pltpu.VMEM((cells, lev), F32)] * 3,
+        *[pltpu.VMEM((cells, lev), F32)] * 2,
         pltpu.VMEM((1, lev), F32),
         *[pltpu.VMEM((lev, lev), F32)] * 2,
         pltpu.VMEM((2, full), jnp.int32),
         *[pltpu.VMEM((2 * lev, 2 * lev), BF16)] * 4,
-        pltpu.VMEM((ITERS, cells + 16, lev), F32),
-        pltpu.VMEM((ITERS, cells, lev), F32),
         pltpu.VMEM((cells, lev), F32),
         *[pltpu.VMEM((ITERS, rows, lev), F32)] * 2,
         *[pltpu.VMEM((ITERS, cols, lev), F32)] * 2,
@@ -643,15 +655,16 @@
         dma((2,)), dma((2,)), dma, dma, dma, dma,
         dma, dma, dma, dma, pltpu.SemaphoreType.REGULAR,
     ]
-    x, res, sq = pl.pallas_call(
+    state = pl.pallas_call(
         functools.partial(kernel, n_gx, n_gy, ny, rows, cols),
         out_shape=(
             pltpu.VMEM((cells, lev), F32),
-            pltpu.VMEM((cells, lev), F32),
-            pltpu.VMEM((1, lev), F32),
+            pltpu.VMEM((ITERS, cells + 16, lev), F32),
+            pltpu.VMEM((ITERS, cells, lev), F32),
+            pltpu.VMEM((2 * ITERS, lev), F32),
         ),
         in_specs=[hbm, hbm, hbm, hbm, hbm, hbm],
-        out_specs=(vmem, vmem, vmem),
+        out_specs=(vmem, vmem, vmem, vmem),
         scratch_shapes=scratch,
         compiler_params=pltpu.CompilerParams(collective_id=0, has_side_effects=True),
         name="solve",
@@ -663,11 +676,11 @@
             jax.ShapeDtypeStruct((cells, lev), F32),
             jax.ShapeDtypeStruct((ITERS,), F32),
         ),
-        in_specs=[vmem, vmem, vmem],
+        in_specs=[vmem, vmem, vmem, vmem],
         out_specs=(hbm, hbm, hbm),
-        scratch_shapes=[pltpu.SMEM((ITERS,), F32), dma((3,))],
+        scratch_shapes=[pltpu.VMEM((cells, lev), F32), pltpu.VMEM((cells, lev), F32), pltpu.SMEM((ITERS,), F32), dma((9,))],
         name="put",
-    )(*[pltpu.with_memory_space_constraint(a, pltpu.VMEM) for a in (x, res, sq)])
+    )(*[pltpu.with_memory_space_constraint(a, pltpu.VMEM) for a in state])
     return x.reshape(rows, cols, lev), res.reshape(rows, cols, lev), sq
 
 

time: 32.5 us -> 32.3 us (level)
  no operation moved by 1% of the time
where the time goes in v7:
time: 32.3 us; the launch traced here: 32.2 us
  Pallas kernels  31.6 us (98%)
  between operations  0.64 us (2%)
    pallas_call x1, Pallas kernels, on_device(): pl.pallas_call(functools.partial(kernel, n_gx, n_gy, ny, rows, cols), out...  30.7 us
    pallas_call x1, Pallas kernels, on_device(): pl.pallas_call(write_out, out_shape=(jax.ShapeDtypeStruct((cells, lev), F...  0.88 us

profile of v7, /device:TPU:1, one launch (start us, length us, event | category | flops | bytes accessed | tf_op | source)
XLA Modules:
  0.0 32.2 jit_solution(2360686568407643892)
XLA Ops:
  0.6 30.7 %solve.1 = (f32[512,128]{1,0:T(8,128)S(1)}, f32[3,528,128]{2,1,0:T(8,128)S(1)}, f32[3,512,128]{2,1,0:T(8,128)S(1)}, f32[6,128]{1,0:T(8,128)S(1)}) custom-call(f32[512,128]{1,0:T(8,128)} %bitcast.6, f32[512,128]{1,0:T(8,128)} %bitcast.7, f32[512,128]{1,0:T(8,128)} %bitcast.8, f32[1,128]{1,0:T(1,128)} %bitcast.9, f32[2,128,128]{2,1,0:T(8,128)} %m_hbm.1, ...), custom_call_target="tpu_custom_call" | custom-call | tf_op jit(solution)/shard_map/solve/pallas_call | solution.py:658
  31.3 0.9 %put.1 = (f32[512,128]{1,0:T(8,128)}, f32[512,128]{1,0:T(8,128)}, f32[3]{0:T(128)}) custom-call(f32[512,128]{1,0:T(8,128)S(1)} %get-tuple-element.10.r_v, f32[3,528,128]{2,1,0:T(8,128)S(1)} %get-tuple-element.11.z_v, f32[3,512,128]{2,1,0:T(8,128)S(1)} %get-tuple-element.12.u_v, f32[6,128]{1,0:T(8,128)S(1)} %get-tuple-element.13.fin), custom_call_target="tpu_custom_call" | custom-call | tf_op jit(solution)/shard_map/put/pallas_call | solution.py:672

commit v8 on v7

--- a/solution.py
+++ b/solution.py
@@ -267,13 +267,11 @@
     for step in range(ITERS):
         src = r_v if step == 0 else u_v.at[step - 1]
         edge_rows_in = jnp.concatenate(
-            [src[last, :], src[first, :], src[cells - cols :, :], src[0:cols, :]], 0
+            [src[last, :], src[first, :]], 0
         )
         bnd = times(edge_rows_in, lev)
         send_e[step] = bnd[0:rows]
         send_w[step] = bnd[rows : 2 * rows]
-        send_n[step] = bnd[2 * rows : 2 * rows + cols]
-        send_s[step] = bnd[2 * rows + cols :]
 
         if step == 0:
             outer = jnp.logical_or(y_ == 0, y_ == ny - 1)
@@ -305,6 +303,9 @@
             for i in range(1, nz):
                 pl.semaphore_signal(ready, inc=1, device_id=at_line(lax.rem(z_ + i, nz)), device_id_type=MESH)
 
+        ends = times(jnp.concatenate([src[cells - cols :, :], src[0:cols, :]], 0), lev)
+        send_n[step] = ends[:cols]
+        send_s[step] = ends[cols:]
         north = pltpu.make_async_remote_copy(
             src_ref=send_n.at[step], dst_ref=hal_s.at[step],
             send_sem=ss_n.at[step], recv_sem=rs_s.at[step],

time: 32.3 us -> 32.3 us (level)
  no operation moved by 1% of the time
where the time goes in v8:
time: 32.3 us; the launch traced here: 32.2 us
  Pallas kernels  31.6 us (98%)
  between operations  0.64 us (2%)
    pallas_call x1, Pallas kernels, on_device(): pl.pallas_call(functools.partial(kernel, n_gx, n_gy, ny, rows, cols), out...  30.7 us
    pallas_call x1, Pallas kernels, on_device(): pl.pallas_call(write_out, out_shape=(jax.ShapeDtypeStruct((cells, lev), F...  0.88 us

profile of v8, /device:TPU:1, one launch (start us, length us, event | category | flops | bytes accessed | tf_op | source)
XLA Modules:
  0.0 32.2 jit_solution(2125715352809786113)
XLA Ops:
  0.6 30.7 %solve.1 = (f32[512,128]{1,0:T(8,128)S(1)}, f32[3,528,128]{2,1,0:T(8,128)S(1)}, f32[3,512,128]{2,1,0:T(8,128)S(1)}, f32[6,128]{1,0:T(8,128)S(1)}) custom-call(f32[512,128]{1,0:T(8,128)} %bitcast.6, f32[512,128]{1,0:T(8,128)} %bitcast.7, f32[512,128]{1,0:T(8,128)} %bitcast.8, f32[1,128]{1,0:T(1,128)} %bitcast.9, f32[2,128,128]{2,1,0:T(8,128)} %m_hbm.1, ...), custom_call_target="tpu_custom_call" | custom-call | tf_op jit(solution)/shard_map/solve/pallas_call | solution.py:659
  31.3 0.9 %put.1 = (f32[512,128]{1,0:T(8,128)}, f32[512,128]{1,0:T(8,128)}, f32[3]{0:T(128)}) custom-call(f32[512,128]{1,0:T(8,128)S(1)} %get-tuple-element.10.r_v, f32[3,528,128]{2,1,0:T(8,128)S(1)} %get-tuple-element.11.z_v, f32[3,512,128]{2,1,0:T(8,128)S(1)} %get-tuple-element.12.u_v, f32[6,128]{1,0:T(8,128)S(1)} %get-tuple-element.13.fin), custom_call_target="tpu_custom_call" | custom-call | tf_op jit(solution)/shard_map/put/pallas_call | solution.py:673
